TPU v7x, 32 devices: a whole 2x2x4 slice. The times are simulated.
32 devices in a mesh: sub: 8 (over z, y), grp: 4 (over x, core).
Axes of the slice: x: 2, y: 2, z: 4, core: 2. Of those that a mesh axis runs over, the one named last changes fastest.
Arguments:
- rr_inverse: float32 [64, 512, 512], P(('sub', 'grp')), may hold values from -4 to 4, as said below
- corner_modes: float32 [64, 64, 512], P(('sub', 'grp')), may hold values from -0.5 to 0.5
- coarse_inverse: float32 [2048, 2048], P(('sub', 'grp')), may hold values from -1 to 1, as said below
- inertia: float32 [64, 512], P(('sub', 'grp')), may hold values from 0.5 to 2
- disp_now: float32 [8, 64, 512], P(None, ('sub', 'grp')), may hold values from -4 to 4
- vel_now: float32 [8, 64, 512], P(None, ('sub', 'grp')), may hold values from -4 to 4
- acc_now: float32 [8, 64, 512], P(None, ('sub', 'grp')), may hold values from -8 to 8
- load_next: float32 [8, 64, 512], P(None, ('sub', 'grp')), may hold values from -10 to 10
- basis_rows: float32 [32768, 256], P(('sub', 'grp')), may hold values from -0.03125 to 0.03125
- piece_owner: int32 [32], replicated, may hold values from 0 to 31, each once
Outputs:
- disp_new: float32 [8, 64, 512], P(None, ('sub', 'grp'))
- vel_new: float32 [8, 64, 512], P(None, ('sub', 'grp'))
- projection: float32 [256, 8], replicated
- r_factor: float32 [8, 8], replicated
- new_columns: float32 [8, 32768], P(None, ('sub', 'grp'))
Inputs may be any that keep to these rules, and one draw needn't show every extreme that they name: piece_owner is a permutation. `rr_inverse`: each of the 64 blocks is symmetric positive definite. `coarse_inverse`: symmetric positive definite.
All inputs are finite; a program needn't handle non-finite values.
Results may differ from a plain program's by a relative error of at most 0.00018.
Values sent between devices are 32-bit elements; how exact they have to be, the bound alone decides.
A program may use at most 64 MiB of HBM per device.

v0:
```python
import functools
import math

import jax
import jax.numpy as jnp
from jax import lax
from jax.experimental import pallas as pl
from jax.experimental.pallas import tpu as pltpu
from jax.sharding import PartitionSpec as P

NC = 32
NI = 128
LANES = 128

time_step = 0.5
newmark_beta = 0.25
newmark_gamma = 0.5

MESH = pl.DeviceIdType.MESH


def nn(a, b):
    return lax.dot_general(
        a, b, (((1,), (0,)), ((), ())), precision=lax.Precision.HIGHEST, preferred_element_type=jnp.float32
    )


def nt(a, b):
    return lax.dot_general(
        a, b, (((1,), (1,)), ((), ())), precision=lax.Precision.HIGHEST, preferred_element_type=jnp.float32
    )


def split(x):
    first = x.astype(jnp.bfloat16)
    rest = x - first.astype(jnp.float32)
    second = rest.astype(jnp.bfloat16)
    return first, second, (rest - second.astype(jnp.float32)).astype(jnp.bfloat16)


def keep_split(parts, matrix):
    for at, part in enumerate(split(matrix)):
        parts[at] = part


def split_dot(x, parts, contracted):
    first, second, third = split(x)
    stacked = jnp.concatenate([first, second, third, jnp.zeros_like(first)], axis=0)
    rows = x.shape[0]

    def product(a, b):
        return lax.dot_general(a, b, (((1,), (contracted,)), ((), ())), preferred_element_type=jnp.float32)

    large = product(stacked, parts[0])
    middle = product(stacked[: 2 * rows], parts[1])
    small = product(stacked[: 2 * rows], parts[2])
    correction = large[2 * rows : 3 * rows] + middle[rows : 2 * rows] + small[:rows]
    return large[:rows] + (large[rows : 2 * rows] + middle[:rows] + correction)


def hand_over(*refs):
    half = len(refs) // 2
    for source, target in zip(refs[:half], refs[half:]):
        target[...] = source[...]


def kernel(
    n,
    groups,
    inner,
    owner_hbm,
    rr_hbm,
    modes_hbm,
    coarse_hbm,
    basis_hbm,
    inertia_hbm,
    disp_hbm,
    vel_hbm,
    acc_hbm,
    load_hbm,
    disp_out,
    vel_out,
    proj_out,
    r_out,
    cols_out,
    owner,
    inverse,
    inertia,
    disp_now,
    vel_now,
    acc_now,
    load_next,
    coarse_parts,
    inter_parts,
    basis_parts,
    rr,
    modes,
    coarse,
    basis,
    modes_next,
    rr_next,
    corner,
    inter,
    gathered,
    edge,
    edge_out,
    norms,
    pieces,
    outgoing,
    incoming,
    proj_parts,
    proj_sums,
    gram_parts,
    green,
    local_sem,
    const_send,
    const_recv,
    wide_send,
    wide_recv,
    edge_send,
    edge_recv,
):
    sub_count, unknowns = rr.shape[0], rr.shape[1]
    rows = sub_count * NC
    me = lax.axis_index("sub") * groups + lax.axis_index("grp")
    following = lax.rem(me + 1, n)
    earlier = lax.rem(me + n - 1, n)

    def device(rank):
        return (rank // groups, lax.rem(rank, groups))

    def others(body):
        def step(i, carry):
            body(lax.rem(me + i, n))
            return carry

        lax.fori_loop(1, n, step, 0)

    def remote(src, dst, send, recv, rank):
        return pltpu.make_async_remote_copy(
            src_ref=src, dst_ref=dst, send_sem=send, recv_sem=recv, device_id=device(rank), device_id_type=MESH
        )

    barrier = pltpu.get_barrier_semaphore()
    others(lambda rank: pl.semaphore_signal(barrier, inc=1, device_id=device(rank), device_id_type=MESH))

    load_rr = pltpu.make_async_copy(rr_hbm, rr, local_sem.at[0])
    load_modes = pltpu.make_async_copy(modes_hbm, modes, local_sem.at[1])
    load_coarse = pltpu.make_async_copy(coarse_hbm, coarse.at[pl.ds(0, rows)], local_sem.at[2])
    load_basis = pltpu.make_async_copy(basis_hbm, basis, local_sem.at[3])
    fields_in = [
        pltpu.make_async_copy(source, target, local_sem.at[4 + at])
        for at, (source, target) in enumerate(
            (
                (inertia_hbm, inertia),
                (disp_hbm, disp_now),
                (vel_hbm, vel_now),
                (acc_hbm, acc_now),
                (load_hbm, load_next),
            )
        )
    ]
    load_owner = pltpu.make_async_copy(owner_hbm, owner, local_sem.at[9])
    load_modes.start()
    for copy in fields_in:
        copy.start()
    load_owner.start()
    load_rr.start()
    load_coarse.start()
    load_basis.start()

    lane = lax.broadcasted_iota(jnp.int32, (8, LANES), 1)
    sublane = lax.broadcasted_iota(jnp.int32, (8, LANES), 0)

    def right_side(k):
        return load_next[:, k, :] + inertia[k : k + 1, :] * (
            disp_now[:, k, :]
            + time_step * vel_now[:, k, :]
            + (0.5 - newmark_beta) * time_step * time_step * acc_now[:, k, :]
        )

    for copy in fields_in:
        copy.wait()
    sides = [right_side(k) for k in range(sub_count)]

    corner[...] = jnp.zeros_like(corner)
    load_modes.wait()
    corner[0:NC, 0:unknowns] = modes[0, NC:, :]
    corner[0:NC, unknowns:] = modes[1, :NC, :]
    corner[NC : 2 * NC, unknowns:] = modes[1, NC:, :]
    corner[3 * NC :, 0:unknowns] = modes[0, :NC, :]

    odd = lax.rem(me, 2) == 1

    def placed(tile):
        return jnp.where(odd, pltpu.roll(tile, 64, 1), tile)

    def broadcast(buffer, at, sem):
        def send(rank):
            remote(buffer.at[at, me], buffer.at[at, me], wide_send.at[sem], wide_recv.at[sem], rank).start()

        others(send)

    def all_but_one(buffer, at, sem):
        return pltpu.make_async_copy(buffer.at[at, pl.ds(0, n - 1)], buffer.at[at, pl.ds(0, n - 1)], sem)

    gathered[0, me] = placed(nt(jnp.concatenate(sides, axis=1), corner[...]))

    pl.semaphore_wait(barrier, n - 1)
    broadcast(gathered, 0, 0)

    constants = [
        remote(coarse_hbm.at[pl.ds(0, NC)], coarse.at[pl.ds(rows, NC)], const_send.at[0], const_recv.at[0], earlier),
        remote(
            coarse_hbm.at[pl.ds(rows - NC, NC)],
            coarse.at[pl.ds(rows + NC, NC)],
            const_send.at[1],
            const_recv.at[1],
            following,
        ),
        remote(modes_hbm.at[0, :, pl.ds(0, NI)], modes_next, const_send.at[2], const_recv.at[2], earlier),
        remote(
            rr_hbm.at[0, pl.ds(0, NI), pl.ds(0, NI)],
            rr_next.at[pl.ds(0, NI)],
            const_send.at[3],
            const_recv.at[3],
            earlier,
        ),
        remote(
            rr_hbm.at[0, pl.ds(unknowns - NI, NI), pl.ds(0, NI)],
            rr_next.at[pl.ds(NI, NI)],
            const_send.at[4],
            const_recv.at[4],
            earlier,
        ),
    ]
    for copy in constants:
        copy.start()

    load_rr.wait()
    local = [nn(sides[k], rr[k]) for k in range(sub_count)]
    edge_out[0] = local[0][:, :NI]
    edges = [remote(edge_out.at[0], edge.at[0], edge_send.at[0], edge_recv.at[0], earlier)]
    edges[0].start()

    load_coarse.wait()
    for copy in constants:
        copy.wait_recv()
    inter[...] = jnp.zeros_like(inter)
    inter[0:NC, 0:NI] = modes[0, NC:, unknowns - NI :] - modes[1, :NC, :NI]
    inter[0:NC, NI:] = modes[1, :NC, unknowns - NI :]
    inter[NC : 2 * NC, 0:NI] = -modes[1, NC:, :NI]
    inter[NC : 2 * NC, NI:] = modes[1, NC:, unknowns - NI :] - modes_next[:NC, :]
    inter[2 * NC : 3 * NC, NI:] = -modes_next[NC:, :]
    inter[3 * NC :, 0:NI] = modes[0, :NC, unknowns - NI :]

    keep_split(inter_parts, inter[...])
    keep_split(coarse_parts, coarse[...])
    load_owner.wait()

    def find(t, carry):
        at = jnp.int32(0)
        for p in range(n):
            at = jnp.where(owner[p] == t, p, at)
        inverse[t] = at
        return carry

    lax.fori_loop(0, n, find, 0)

    def coarse_solve(at):
        all_but_one(gathered, at, wide_recv.at[at]).wait()
        assembled = []
        for j in range(n // 2):
            low = jnp.where(lane < 96, gathered[at, 2 * j], gathered[at, (2 * j + 2) % n])
            high = jnp.where(lane >= 32, gathered[at, 2 * j + 1], gathered[at, (2 * j - 1) % n])
            assembled.append(low + high)
        return split_dot(jnp.concatenate(assembled, axis=1), coarse_parts, 1)

    def jumps(fields, next_first):
        firsts = [field[:, :NI] for field in fields[1:]] + [next_first]
        return jnp.concatenate(
            [field[:, unknowns - NI :] - first for field, first in zip(fields, firsts)], axis=1
        )

    per_piece = unknowns // n
    width = sub_count * per_piece

    def piece_part(fields, which, p):
        block = p * per_piece // LANES
        inside = p * per_piece % LANES
        part = jnp.zeros((8, LANES), jnp.float32)
        for k in range(sub_count):
            target = which * width + k * per_piece
            rolled = pltpu.roll(
                fields[k][:, block * LANES : (block + 1) * LANES], (target - inside) % LANES, 1
            )
            part = jnp.where((lane >= target) & (lane < target + per_piece), rolled, part)
        return part

    solved = coarse_solve(0)
    edges[0].wait_recv()
    vector0 = jumps(local, edge[0]) + split_dot(solved, inter_parts, 0)

    def start_image(vector, at):
        gathered[at, me] = placed(split_dot(vector, inter_parts, 1))
        broadcast(gathered, at, at)
        slot = 2 * at - 1
        edge_out[slot] = vector[:, NI:]
        edge_out[slot + 1] = vector[:, :NI]
        for offset, rank in ((0, following), (1, earlier)):
            copy = remote(
                edge_out.at[slot + offset],
                edge.at[slot + offset],
                edge_send.at[slot + offset],
                edge_recv.at[slot + offset],
                rank,
            )
            copy.start()
            edges.append(copy)

    def end_image(vector, at):
        slot = 2 * at - 1
        head, tail = vector[:, :NI], vector[:, NI:]
        second = nn(-head, rr[1, :NI, :]) + nn(tail, rr[1, unknowns - NI :, :])
        edges[slot].wait_recv()
        edges[slot + 1].wait_recv()
        first = nn(-edge[slot], rr[0, :NI, :]) + nn(head, rr[0, unknowns - NI :, :])
        beyond = nn(-tail, rr_next[:NI, :]) + nn(edge[slot + 1], rr_next[NI:, :])
        inside = [first, second]
        values = coarse_solve(at)
        return inside, values, jumps(inside, beyond) + split_dot(values, inter_parts, 0)

    def with_corners(inside, values):
        return [
            inside[k] + nn(values, corner[:, k * unknowns : (k + 1) * unknowns]) for k in range(sub_count)
        ]

    def column(values):
        return jnp.sum(values, axis=1, keepdims=True)

    start_image(vector0, 1)
    first_fields = with_corners(local, solved)
    for k in range(sub_count):
        green[k] = first_fields[k]
    for p in range(n):
        pieces[p] = piece_part(first_fields, 0, p)
    inside0, values0, vector1 = end_image(vector0, 1)

    start_image(vector1, 2)
    norm_row = jnp.where(lane == sublane, column(vector0 * vector0), 0.0) + jnp.where(
        lane == sublane + 8, column(vector0 * vector1), 0.0
    )
    norms[0, me] = jnp.sum(norm_row, axis=0, keepdims=True)
    broadcast(norms, 0, 3)
    fields0 = with_corners(inside0, values0)
    for p in range(n):
        pieces[p] = pieces[p] + piece_part(fields0, 1, p)
    load_basis.wait()
    keep_split(basis_parts, basis[...])
    inside1, values1, vector2 = end_image(vector1, 2)
    fields1 = with_corners(inside1, values1)

    all_but_one(norms, 0, wide_recv.at[3]).wait()
    totals = jnp.broadcast_to(jnp.sum(norms[0], axis=0), (8, LANES))
    norm0 = column(jnp.where(lane == sublane, totals, 0.0))
    curve0 = column(jnp.where(lane == sublane + 8, totals, 0.0))
    alpha0 = norm0 / curve0
    residual = vector0 - alpha0 * vector1
    residual_image = vector1 - alpha0 * vector2
    extra = (
        jnp.where(lane == 3 * width, column(residual * residual), 0.0)
        + jnp.where(lane == 3 * width + 1, column(residual * residual_image), 0.0)
        + jnp.where(lane == 3 * width + 2, column(residual * vector1), 0.0)
    )
    for p in range(n):
        pieces[p] = pieces[p] + piece_part(fields1, 2, p) + extra
    for t in range(n):
        outgoing[t] = pieces[inverse[t]]

    def send_piece(rank):
        remote(outgoing.at[rank], incoming.at[0, me], wide_send.at[4], wide_recv.at[4], rank).start()

    others(send_piece)
    incoming[0, me] = outgoing[me]
    all_but_one(incoming, 0, wide_recv.at[4]).wait()

    sums = jnp.sum(incoming[0], axis=0)
    norm1 = column(jnp.where(lane == 3 * width, sums, 0.0))
    curve_rr = column(jnp.where(lane == 3 * width + 1, sums, 0.0))
    curve_rp = column(jnp.where(lane == 3 * width + 2, sums, 0.0))
    beta = norm1 / norm0
    curve1 = curve_rr + 2.0 * beta * curve_rp + beta * beta * curve0
    alpha1 = norm1 / curve1
    scale0 = alpha0 + alpha1 * (1.0 + beta)
    scale1 = -alpha1 * alpha0

    factor = jnp.where(lane < width, 1.0, jnp.where(lane < 2 * width, -scale0, -scale1))
    factor = jnp.where(lane < 3 * width, factor, 0.0)
    per_tile = LANES // width
    snapshot_tiles = []
    for j in range(n // per_tile):
        tile = jnp.zeros((8, LANES), jnp.float32)
        for i in range(per_tile):
            scaled = incoming[0, j * per_tile + i] * factor
            total = scaled
            for which in (1, 2):
                total = total + pltpu.roll(scaled, LANES - which * width, 1)
            if i:
                total = pltpu.roll(total, i * width, 1)
            tile = jnp.where((lane >= i * width) & (lane < (i + 1) * width), total, tile)
        snapshot_tiles.append(tile)
    snapshots = jnp.concatenate(snapshot_tiles, axis=1)
    plane, outer = me // inner, n // inner
    seat = lax.rem(me, inner)
    proj_parts[seat] = split_dot(snapshots, basis_parts, 0)
    for i in range(1, inner):
        rank = plane * inner + lax.rem(seat + i, inner)
        remote(proj_parts.at[seat], proj_parts.at[seat], wide_send.at[5], wide_recv.at[5], rank).start()

    for k in range(sub_count):
        carried = green[k] - scale0 * fields0[k] - scale1 * fields1[k]
        now, vel, acc = disp_now[:, k, :], vel_now[:, k, :], acc_now[:, k, :]
        accel_new = (
            (carried - now) / (newmark_beta * time_step * time_step)
            - vel / (newmark_beta * time_step)
            - (0.5 / newmark_beta - 1.0) * acc
        )
        disp_out[:, k, :] = carried
        vel_out[:, k, :] = vel + time_step * ((1.0 - newmark_gamma) * acc + newmark_gamma * accel_new)

    pltpu.make_async_copy(
        proj_parts.at[pl.ds(0, inner - 1)], proj_parts.at[pl.ds(0, inner - 1)], wide_recv.at[5]
    ).wait()
    proj_sums[plane] = jnp.sum(proj_parts[...], axis=0)
    for i in range(1, outer):
        rank = lax.rem(plane + i, outer) * inner + seat
        remote(proj_sums.at[plane], proj_sums.at[plane], wide_send.at[7], wide_recv.at[7], rank).start()
    pltpu.make_async_copy(
        proj_sums.at[pl.ds(0, outer - 1)], proj_sums.at[pl.ds(0, outer - 1)], wide_recv.at[7]
    ).wait()
    projection = jnp.sum(proj_sums[...], axis=0)
    proj_out[...] = projection
    remainder = snapshots - split_dot(projection, basis_parts, 1)
    repeated = jnp.concatenate([remainder] * (LANES // 8), axis=0)
    gram_wide = nt(remainder, repeated)
    gram_parts[0, me] = jnp.sum(
        jnp.where(lane // 8 == sublane, gram_wide, 0.0), axis=0, keepdims=True
    )
    broadcast(gram_parts, 0, 6)
    all_but_one(gram_parts, 0, wide_recv.at[6]).wait()
    gram_row = jnp.broadcast_to(jnp.sum(gram_parts[0], axis=0), (8, LANES))
    work = gram_row
    for i in range(1, 8):
        work = jnp.where(sublane == i, pltpu.roll(gram_row, LANES - 8 * i, 1), work)
    for j in range(8):
        inverse_root = lax.rsqrt(work[j : j + 1, j : j + 1])
        pivot = work[j : j + 1, :] * inverse_root
        below = work[:, j : j + 1] * inverse_root
        pivot_rows = remainder[j : j + 1, :] * inverse_root
        work = jnp.where(sublane == j, pivot, jnp.where(sublane > j, work - below * pivot, work))
        row_at = lax.broadcasted_iota(jnp.int32, remainder.shape, 0)
        remainder = jnp.where(
            row_at == j, pivot_rows, jnp.where(row_at > j, remainder - below * pivot_rows, remainder)
        )
    scale_rows = math.sqrt(snapshots.shape[1] * n)
    r_out[...] = jnp.where(lane >= sublane, work, 0.0)[:, :8] * (1.0 / scale_rows)
    cols_out[...] = remainder * scale_rows

    for copy in constants + edges:
        copy.wait_send()
    for at in range(3):
        all_but_one(gathered, at, wide_send.at[at]).wait()
    all_but_one(norms, 0, wide_send.at[3]).wait()
    all_but_one(incoming, 0, wide_send.at[4]).wait()
    pltpu.make_async_copy(
        proj_parts.at[pl.ds(0, inner - 1)], proj_parts.at[pl.ds(0, inner - 1)], wide_send.at[5]
    ).wait()
    pltpu.make_async_copy(
        proj_sums.at[pl.ds(0, outer - 1)], proj_sums.at[pl.ds(0, outer - 1)], wide_send.at[7]
    ).wait()
    all_but_one(gram_parts, 0, wide_send.at[6]).wait()


def solution(mesh):
    groups = mesh.shape["grp"]
    n = mesh.shape["sub"] * groups
    inner = math.gcd(n, 8)

    def shards(
        rr_inverse,
        corner_modes,
        coarse_inverse,
        inertia,
        disp_now,
        vel_now,
        acc_now,
        load_next,
        basis_rows,
        piece_owner,
    ):
        case_count, sub_count, unknowns = disp_now.shape
        rank = basis_rows.shape[1]
        local_rows = basis_rows.shape[0]
        width = (sub_count + 2) * NC
        f32 = jnp.float32
        vmem = pl.BlockSpec(memory_space=pltpu.VMEM)
        anywhere = pl.BlockSpec(memory_space=pl.ANY)
        results = (
            jax.ShapeDtypeStruct(disp_now.shape, f32),
            jax.ShapeDtypeStruct(disp_now.shape, f32),
            jax.ShapeDtypeStruct((case_count, rank), f32),
            jax.ShapeDtypeStruct((case_count, case_count), f32),
            jax.ShapeDtypeStruct((case_count, local_rows), f32),
        )
        computed = pl.pallas_call(
            functools.partial(kernel, n, groups, inner),
            out_shape=results,
            in_specs=[anywhere] * 10,
            out_specs=(vmem,) * 5,
            scratch_shapes=[
                pltpu.SMEM(piece_owner.shape, jnp.int32),
                pltpu.SMEM(piece_owner.shape, jnp.int32),
                pltpu.VMEM(inertia.shape, f32),
                pltpu.VMEM(disp_now.shape, f32),
                pltpu.VMEM(vel_now.shape, f32),
                pltpu.VMEM(acc_now.shape, f32),
                pltpu.VMEM(load_next.shape, f32),
                pltpu.VMEM((3, width, coarse_inverse.shape[1]), jnp.bfloat16),
                pltpu.VMEM((3, width, sub_count * NI), jnp.bfloat16),
                pltpu.VMEM((3,) + basis_rows.shape, jnp.bfloat16),
                pltpu.VMEM(rr_inverse.shape, f32),
                pltpu.VMEM(corner_modes.shape, f32),
                pltpu.VMEM((width, coarse_inverse.shape[1]), f32),
                pltpu.VMEM(basis_rows.shape, f32),
                pltpu.VMEM((2 * NC, NI), f32),
                pltpu.VMEM((2 * NI, NI), f32),
                pltpu.VMEM((width, sub_count * unknowns), f32),
                pltpu.VMEM((width, sub_count * NI), f32),
                pltpu.VMEM((3, n, case_count, width), f32),
                pltpu.VMEM((5, case_count, NI), f32),
                pltpu.VMEM((5, case_count, NI), f32),
                pltpu.VMEM((1, n, 1, LANES), f32),
                pltpu.VMEM((n, case_count, LANES), f32),
                pltpu.VMEM((n, case_count, LANES), f32),
                pltpu.VMEM((1, n, case_count, LANES), f32),
                pltpu.VMEM((inner, case_count, rank), f32),
                pltpu.VMEM((n // inner, case_count, rank), f32),
                pltpu.VMEM((1, n, 1, LANES), f32),
                pltpu.VMEM((sub_count, case_count, unknowns), f32),
                pltpu.SemaphoreType.DMA((10,)),
                pltpu.SemaphoreType.DMA((5,)),
                pltpu.SemaphoreType.DMA((5,)),
                pltpu.SemaphoreType.DMA((8,)),
                pltpu.SemaphoreType.DMA((8,)),
                pltpu.SemaphoreType.DMA((5,)),
                pltpu.SemaphoreType.DMA((5,)),
            ],
            compiler_params=pltpu.CompilerParams(collective_id=0, has_side_effects=True),
        )(
            piece_owner,
            rr_inverse,
            corner_modes,
            coarse_inverse,
            basis_rows,
            inertia,
            disp_now,
            vel_now,
            acc_now,
            load_next,
        )
        disp, vel, proj, r_factor, columns = pl.pallas_call(
            hand_over, out_shape=results, in_specs=[vmem] * 5, out_specs=(vmem,) * 5
        )(*computed)
        return disp, vel, proj.T, r_factor, columns

    return jax.shard_map(
        shards,
        mesh=mesh,
        in_specs=(
            P(("sub", "grp"), None, None),
            P(("sub", "grp"), None, None),
            P(("sub", "grp"), None),
            P(("sub", "grp"), None),
            P(None, ("sub", "grp"), None),
            P(None, ("sub", "grp"), None),
            P(None, ("sub", "grp"), None),
            P(None, ("sub", "grp"), None),
            P(("sub", "grp"), None),
            P(),
        ),
        out_specs=(
            P(None, ("sub", "grp"), None),
            P(None, ("sub", "grp"), None),
            P(),
            P(),
            P(None, ("sub", "grp")),
        ),
        check_vma=False,
    )
```

profile of v0, /device:TPU:0, one launch (start us, length us, event | category | flops | bytes accessed | tf_op | source)
XLA Modules:
  0.0 55.5 jit_solution(14557732303557705080)
XLA Ops:
  0.6 53.4 %shard_map.137 = (f32[8,2,512]{2,1,0:T(2,128)}, f32[8,2,512]{2,1,0:T(2,128)}, f32[8,256]{1,0:T(8,128)}, f32[8,8]{1,0:T(8,128)}, f32[8,1024]{1,0:T(8,128)}) custom-call(s32[32]{0:T(128)} %owner_hbm.1, f32[2,512,512]{2,1,0:T(8,128)} %rr_hbm.1, f32[2,64,512]{2,1,0:T(8,128)} %modes_hbm.1, f32[64,2048]{1,0:T(8,128)} %coarse_hbm.1, f32[1024,256]{1,0:T(8,128)} %basis_hbm.1, ...), custom_call_target="tpu_custom_call" | custom-call | tf_op jit(solution)/shard_map/pallas_call | solution.py:515
  54.1 1.5 %shard_map.138 = (f32[8,2,512]{2,1,0:T(2,128)}, f32[8,2,512]{2,1,0:T(2,128)}, f32[8,256]{1,0:T(8,128)}, f32[8,8]{1,0:T(8,128)}, f32[8,1024]{1,0:T(8,128)}) custom-call(f32[8,2,512]{2,1,0:T(2,128)} %get-tuple-element.15.refs_0_, f32[8,2,512]{2,1,0:T(2,128)} %get-tuple-element.16.refs_1_, f32[8,256]{1,0:T(8,128)} %get-tuple-element.17.refs_2_, ...), custom_call_target="tpu_custom_call" | custom-call | tf_op jit(solution)/shard_map/pallas_call | solution.py:571
where the time goes:
time: 55.7 us; the launch traced here: 55.5 us
  Pallas kernels  54.9 us (99%)
  between operations  0.64 us (1%)
    pallas_call x1, Pallas kernels, shards(): pl.pallas_call(functools.partial(kernel, n, groups, inner), out_shape=res...  53.4 us
    pallas_call x1, Pallas kernels, shards(): pl.pallas_call(hand_over, out_shape=results, in_specs=[vmem] * 5, out_spe...  1.46 us

commit v1 on v0

--- a/solution.py
+++ b/solution.py
@@ -91,16 +91,18 @@
     acc_now,
     load_next,
     coarse_parts,
-    inter_parts,
+    forward_parts,
+    backward_parts,
     basis_parts,
     rr,
     modes,
     coarse,
     basis,
     modes_next,
-    rr_next,
+    modes_prev,
     corner,
-    inter,
+    forward,
+    backward,
     gathered,
     edge,
     edge_out,
@@ -125,16 +127,33 @@
     me = lax.axis_index("sub") * groups + lax.axis_index("grp")
     following = lax.rem(me + 1, n)
     earlier = lax.rem(me + n - 1, n)
+    odd = lax.rem(me, 2) == 1
+    partner = jnp.where(odd, earlier, following)
+    outward = jnp.where(odd, following, earlier)
 
     def device(rank):
         return (rank // groups, lax.rem(rank, groups))
 
+    plane, outer = me // inner, n // inner
+    seat = lax.rem(me, inner)
+    seats = [lax.rem(2 * inner - 1 - seat + i, inner) for i in range(inner)]
+    mirrored = 2 * plane > outer - 1
+    depth = jnp.where(mirrored, outer - 1 - plane, plane)
+    lead = outer - 1 - 2 * depth
+
     def others(body):
         def step(i, carry):
-            body(lax.rem(me + i, n))
+            beyond = i - lead
+            turn = jnp.where(lax.rem(beyond, 2) == 0, 2 * depth - beyond // 2, beyond // 2)
+            at = jnp.where(i < lead, outer - 1 - i, turn)
+            at = jnp.where(mirrored, outer - 1 - at, at)
+            for there in seats:
+                body(at * inner + there)
             return carry
 
-        lax.fori_loop(1, n, step, 0)
+        lax.fori_loop(0, outer - 1, step, 0)
+        for i in range(1, inner):
+            body(plane * inner + lax.rem(seat + i, inner))
 
     def remote(src, dst, send, recv, rank):
         return pltpu.make_async_remote_copy(
@@ -165,8 +184,8 @@
     for copy in fields_in:
         copy.start()
     load_owner.start()
+    load_coarse.start()
     load_rr.start()
-    load_coarse.start()
     load_basis.start()
 
     lane = lax.broadcasted_iota(jnp.int32, (8, LANES), 1)
@@ -190,8 +209,6 @@
     corner[NC : 2 * NC, unknowns:] = modes[1, NC:, :]
     corner[3 * NC :, 0:unknowns] = modes[0, :NC, :]
 
-    odd = lax.rem(me, 2) == 1
-
     def placed(tile):
         return jnp.where(odd, pltpu.roll(tile, 64, 1), tile)
 
@@ -209,53 +226,30 @@
     pl.semaphore_wait(barrier, n - 1)
     broadcast(gathered, 0, 0)
 
-    constants = [
-        remote(coarse_hbm.at[pl.ds(0, NC)], coarse.at[pl.ds(rows, NC)], const_send.at[0], const_recv.at[0], earlier),
+    load_coarse.wait()
+    halos = [
         remote(
-            coarse_hbm.at[pl.ds(rows - NC, NC)],
-            coarse.at[pl.ds(rows + NC, NC)],
-            const_send.at[1],
-            const_recv.at[1],
-            following,
+            coarse.at[pl.ds(NC, NC)], coarse.at[pl.ds(3 * NC, NC)], const_send.at[0], const_recv.at[0], following
         ),
-        remote(modes_hbm.at[0, :, pl.ds(0, NI)], modes_next, const_send.at[2], const_recv.at[2], earlier),
-        remote(
-            rr_hbm.at[0, pl.ds(0, NI), pl.ds(0, NI)],
-            rr_next.at[pl.ds(0, NI)],
-            const_send.at[3],
-            const_recv.at[3],
-            earlier,
-        ),
-        remote(
-            rr_hbm.at[0, pl.ds(unknowns - NI, NI), pl.ds(0, NI)],
-            rr_next.at[pl.ds(NI, NI)],
-            const_send.at[4],
-            const_recv.at[4],
-            earlier,
-        ),
+        remote(modes.at[1, :, pl.ds(unknowns - NI, NI)], modes_prev, const_send.at[1], const_recv.at[1], following),
+        remote(modes.at[0, :, pl.ds(0, NI)], modes_next, const_send.at[2], const_recv.at[2], earlier),
+        remote(coarse.at[pl.ds(0, NC)], coarse.at[pl.ds(2 * NC, NC)], const_send.at[3], const_recv.at[3], partner),
     ]
-    for copy in constants:
+    for copy in halos:
         copy.start()
 
     load_rr.wait()
     local = [nn(sides[k], rr[k]) for k in range(sub_count)]
-    edge_out[0] = local[0][:, :NI]
-    edges = [remote(edge_out.at[0], edge.at[0], edge_send.at[0], edge_recv.at[0], earlier)]
-    edges[0].start()
-
-    load_coarse.wait()
-    for copy in constants:
-        copy.wait_recv()
-    inter[...] = jnp.zeros_like(inter)
-    inter[0:NC, 0:NI] = modes[0, NC:, unknowns - NI :] - modes[1, :NC, :NI]
-    inter[0:NC, NI:] = modes[1, :NC, unknowns - NI :]
-    inter[NC : 2 * NC, 0:NI] = -modes[1, NC:, :NI]
-    inter[NC : 2 * NC, NI:] = modes[1, NC:, unknowns - NI :] - modes_next[:NC, :]
-    inter[2 * NC : 3 * NC, NI:] = -modes_next[NC:, :]
-    inter[3 * NC :, 0:NI] = modes[0, :NC, unknowns - NI :]
-
-    keep_split(inter_parts, inter[...])
-    keep_split(coarse_parts, coarse[...])
+    def facing_edge(first, last, at):
+        edge_out[at] = jnp.where(odd, first, last)
+        copy = remote(edge_out.at[at], edge.at[at], edge_send.at[at], edge_recv.at[at], partner)
+        copy.start()
+        edges.append(copy)
+        return copy
+
+    edges = []
+    met = facing_edge(local[0][:, :NI], local[1][:, unknowns - NI :], 0)
+
     load_owner.wait()
 
     def find(t, carry):
@@ -266,21 +260,48 @@
         return carry
 
     lax.fori_loop(0, n, find, 0)
+    for copy in halos:
+        copy.wait_recv()
+    first0, last0 = modes[0, :, :NI], modes[0, :, unknowns - NI :]
+    first1, last1 = modes[1, :, :NI], modes[1, :, unknowns - NI :]
+    before, after = modes_prev[...], modes_next[...]
+    forward[...] = jnp.zeros_like(forward)
+    forward[0:NC, 0:NI] = -first0[NC:]
+    forward[0:NC, NI : 2 * NI] = last0[NC:] - first1[:NC]
+    forward[0:NC, 2 * NI :] = last1[:NC]
+    forward[NC : 2 * NC, NI : 2 * NI] = -first1[NC:]
+    forward[NC : 2 * NC, 2 * NI :] = last1[NC:] - jnp.where(odd, 0.0, after[:NC])
+    forward[2 * NC : 3 * NC, 0:NI] = jnp.where(odd, before[:NC], 0.0)
+    forward[2 * NC : 3 * NC, 2 * NI :] = jnp.where(odd, 0.0, -after[NC:])
+    forward[3 * NC :, 0:NI] = jnp.where(odd, before[NC:], 0.0) - first0[:NC]
+    forward[3 * NC :, NI : 2 * NI] = last0[:NC]
+    backward[...] = jnp.zeros_like(backward)
+    backward[0:NC, :] = forward[0:NC, :]
+    backward[NC : 2 * NC, NI : 2 * NI] = -first1[NC:]
+    backward[NC : 2 * NC, 2 * NI :] = last1[NC:] - after[:NC]
+    backward[2 * NC : 3 * NC, 0:NI] = jnp.where(odd, 0.0, before[:NC])
+    backward[2 * NC : 3 * NC, 2 * NI :] = jnp.where(odd, -after[NC:], 0.0)
+    backward[3 * NC :, 0:NI] = jnp.where(odd, 0.0, before[NC:] - first0[:NC])
+    backward[3 * NC :, NI : 2 * NI] = last0[:NC]
+
+    keep_split(forward_parts, forward[...])
+    keep_split(backward_parts, backward[...])
+    keep_split(coarse_parts, coarse[...])
 
     def coarse_solve(at):
         all_but_one(gathered, at, wide_recv.at[at]).wait()
         assembled = []
         for j in range(n // 2):
-            low = jnp.where(lane < 96, gathered[at, 2 * j], gathered[at, (2 * j + 2) % n])
+            low = jnp.where(lane < 64, gathered[at, 2 * j], gathered[at, (2 * j + 2) % n])
             high = jnp.where(lane >= 32, gathered[at, 2 * j + 1], gathered[at, (2 * j - 1) % n])
             assembled.append(low + high)
         return split_dot(jnp.concatenate(assembled, axis=1), coarse_parts, 1)
 
-    def jumps(fields, next_first):
-        firsts = [field[:, :NI] for field in fields[1:]] + [next_first]
-        return jnp.concatenate(
-            [field[:, unknowns - NI :] - first for field, first in zip(fields, firsts)], axis=1
-        )
+    def jumps(fields, across):
+        first, second = fields
+        left = jnp.where(odd, across, 0.0) - first[:, :NI]
+        right = second[:, unknowns - NI :] - jnp.where(odd, 0.0, across)
+        return jnp.concatenate([left, first[:, unknowns - NI :] - second[:, :NI], right], axis=1)
 
     per_piece = unknowns // n
     width = sub_count * per_piece
@@ -298,37 +319,50 @@
         return part
 
     solved = coarse_solve(0)
-    edges[0].wait_recv()
-    vector0 = jumps(local, edge[0]) + split_dot(solved, inter_parts, 0)
+    met.wait_recv()
+    vector0 = jumps(local, edge[0]) + split_dot(solved, forward_parts, 0)
 
     def start_image(vector, at):
-        gathered[at, me] = placed(split_dot(vector, inter_parts, 1))
+        gathered[at, me] = placed(split_dot(vector, backward_parts, 1))
         broadcast(gathered, at, at)
         slot = 2 * at - 1
-        edge_out[slot] = vector[:, NI:]
-        edge_out[slot + 1] = vector[:, :NI]
-        for offset, rank in ((0, following), (1, earlier)):
-            copy = remote(
-                edge_out.at[slot + offset],
-                edge.at[slot + offset],
-                edge_send.at[slot + offset],
-                edge_recv.at[slot + offset],
-                rank,
-            )
-            copy.start()
-            edges.append(copy)
-
-    def end_image(vector, at):
-        slot = 2 * at - 1
-        head, tail = vector[:, :NI], vector[:, NI:]
-        second = nn(-head, rr[1, :NI, :]) + nn(tail, rr[1, unknowns - NI :, :])
-        edges[slot].wait_recv()
-        edges[slot + 1].wait_recv()
-        first = nn(-edge[slot], rr[0, :NI, :]) + nn(head, rr[0, unknowns - NI :, :])
-        beyond = nn(-tail, rr_next[:NI, :]) + nn(edge[slot + 1], rr_next[NI:, :])
-        inside = [first, second]
+        edge_out[slot] = jnp.where(odd, vector[:, 2 * NI :], vector[:, :NI])
+        copy = remote(edge_out.at[slot], edge.at[slot], edge_send.at[slot], edge_recv.at[slot], outward)
+        copy.start()
+        edges.append(copy)
+        left, middle, right = vector[:, :NI], vector[:, NI : 2 * NI], vector[:, 2 * NI :]
+        near = rr.at[jnp.where(odd, 0, 1)]
+        facing = nn(jnp.where(odd, -left, -middle), near[:NI, :]) + nn(
+            jnp.where(odd, middle, right), near[unknowns - NI :, :]
+        )
+        return copy, facing_edge(facing[:, :NI], facing[:, unknowns - NI :], slot + 1), facing
+
+    def whole(vector, copy, at):
+        copy.wait_recv()
+        other = edge[2 * at - 1]
+        return jnp.concatenate(
+            [
+                vector[:, :NI] + jnp.where(odd, 0.0, other),
+                vector[:, NI : 2 * NI],
+                vector[:, 2 * NI :] + jnp.where(odd, other, 0.0),
+            ],
+            axis=1,
+        )
+
+    def end_image(full, met, facing, at):
+        left, middle, right = full[:, :NI], full[:, NI : 2 * NI], full[:, 2 * NI :]
+        far = rr.at[jnp.where(odd, 1, 0)]
+        outer_field = nn(jnp.where(odd, -middle, -left), far[:NI, :]) + nn(
+            jnp.where(odd, right, middle), far[unknowns - NI :, :]
+        )
+        inside = [jnp.where(odd, facing, outer_field), jnp.where(odd, outer_field, facing)]
+        met.wait_recv()
+        known = jumps(inside, edge[2 * at])
         values = coarse_solve(at)
-        return inside, values, jumps(inside, beyond) + split_dot(values, inter_parts, 0)
+        return inside, values, known + split_dot(values, forward_parts, 0)
+
+    def counted(vector):
+        return jnp.concatenate([jnp.where(odd, 0.0, vector[:, :NI]), vector[:, NI:]], axis=1)
 
     def with_corners(inside, values):
         return [
@@ -338,17 +372,18 @@
     def column(values):
         return jnp.sum(values, axis=1, keepdims=True)
 
-    start_image(vector0, 1)
+    sent0, met0, facing0 = start_image(vector0, 1)
     first_fields = with_corners(local, solved)
     for k in range(sub_count):
         green[k] = first_fields[k]
     for p in range(n):
         pieces[p] = piece_part(first_fields, 0, p)
-    inside0, values0, vector1 = end_image(vector0, 1)
-
-    start_image(vector1, 2)
-    norm_row = jnp.where(lane == sublane, column(vector0 * vector0), 0.0) + jnp.where(
-        lane == sublane + 8, column(vector0 * vector1), 0.0
+    full0 = whole(vector0, sent0, 1)
+    inside0, values0, vector1 = end_image(full0, met0, facing0, 1)
+
+    sent1, met1, facing1 = start_image(vector1, 2)
+    norm_row = jnp.where(lane == sublane, column(full0 * counted(vector0)), 0.0) + jnp.where(
+        lane == sublane + 8, column(full0 * counted(vector1)), 0.0
     )
     norms[0, me] = jnp.sum(norm_row, axis=0, keepdims=True)
     broadcast(norms, 0, 3)
@@ -357,7 +392,8 @@
         pieces[p] = pieces[p] + piece_part(fields0, 1, p)
     load_basis.wait()
     keep_split(basis_parts, basis[...])
-    inside1, values1, vector2 = end_image(vector1, 2)
+    full1 = whole(vector1, sent1, 2)
+    inside1, values1, vector2 = end_image(full1, met1, facing1, 2)
     fields1 = with_corners(inside1, values1)
 
     all_but_one(norms, 0, wide_recv.at[3]).wait()
@@ -365,12 +401,13 @@
     norm0 = column(jnp.where(lane == sublane, totals, 0.0))
     curve0 = column(jnp.where(lane == sublane + 8, totals, 0.0))
     alpha0 = norm0 / curve0
-    residual = vector0 - alpha0 * vector1
-    residual_image = vector1 - alpha0 * vector2
+    residual = full0 - alpha0 * full1
+    residual_part = counted(vector0 - alpha0 * vector1)
+    residual_image = counted(vector1 - alpha0 * vector2)
     extra = (
-        jnp.where(lane == 3 * width, column(residual * residual), 0.0)
+        jnp.where(lane == 3 * width, column(residual * residual_part), 0.0)
         + jnp.where(lane == 3 * width + 1, column(residual * residual_image), 0.0)
-        + jnp.where(lane == 3 * width + 2, column(residual * vector1), 0.0)
+        + jnp.where(lane == 3 * width + 2, column(residual * counted(vector1)), 0.0)
     )
     for p in range(n):
         pieces[p] = pieces[p] + piece_part(fields1, 2, p) + extra
@@ -410,8 +447,6 @@
             tile = jnp.where((lane >= i * width) & (lane < (i + 1) * width), total, tile)
         snapshot_tiles.append(tile)
     snapshots = jnp.concatenate(snapshot_tiles, axis=1)
-    plane, outer = me // inner, n // inner
-    seat = lax.rem(me, inner)
     proj_parts[seat] = split_dot(snapshots, basis_parts, 0)
     for i in range(1, inner):
         rank = plane * inner + lax.rem(seat + i, inner)
@@ -441,11 +476,13 @@
     projection = jnp.sum(proj_sums[...], axis=0)
     proj_out[...] = projection
     remainder = snapshots - split_dot(projection, basis_parts, 1)
-    repeated = jnp.concatenate([remainder] * (LANES // 8), axis=0)
-    gram_wide = nt(remainder, repeated)
-    gram_parts[0, me] = jnp.sum(
-        jnp.where(lane // 8 == sublane, gram_wide, 0.0), axis=0, keepdims=True
-    )
+    gram_row = jnp.zeros((8, LANES), jnp.float32)
+    for shift in range(5):
+        product = remainder * pltpu.roll(remainder, shift, 0)
+        other = lax.rem(sublane + 8 - shift, 8)
+        here = (lane == 8 * sublane + other) | ((lane == 8 * other + sublane) & (shift < 4))
+        gram_row = jnp.where(here, column(product), gram_row)
+    gram_parts[0, me] = jnp.sum(gram_row, axis=0, keepdims=True)
     broadcast(gram_parts, 0, 6)
     all_but_one(gram_parts, 0, wide_recv.at[6]).wait()
     gram_row = jnp.broadcast_to(jnp.sum(gram_parts[0], axis=0), (8, LANES))
@@ -466,7 +503,7 @@
     r_out[...] = jnp.where(lane >= sublane, work, 0.0)[:, :8] * (1.0 / scale_rows)
     cols_out[...] = remainder * scale_rows
 
-    for copy in constants + edges:
+    for copy in halos + edges:
         copy.wait_send()
     for at in range(3):
         all_but_one(gathered, at, wide_send.at[at]).wait()
@@ -526,16 +563,18 @@
                 pltpu.VMEM(acc_now.shape, f32),
                 pltpu.VMEM(load_next.shape, f32),
                 pltpu.VMEM((3, width, coarse_inverse.shape[1]), jnp.bfloat16),
-                pltpu.VMEM((3, width, sub_count * NI), jnp.bfloat16),
+                pltpu.VMEM((3, width, (sub_count + 1) * NI), jnp.bfloat16),
+                pltpu.VMEM((3, width, (sub_count + 1) * NI), jnp.bfloat16),
                 pltpu.VMEM((3,) + basis_rows.shape, jnp.bfloat16),
                 pltpu.VMEM(rr_inverse.shape, f32),
                 pltpu.VMEM(corner_modes.shape, f32),
                 pltpu.VMEM((width, coarse_inverse.shape[1]), f32),
                 pltpu.VMEM(basis_rows.shape, f32),
                 pltpu.VMEM((2 * NC, NI), f32),
-                pltpu.VMEM((2 * NI, NI), f32),
+                pltpu.VMEM((2 * NC, NI), f32),
                 pltpu.VMEM((width, sub_count * unknowns), f32),
-                pltpu.VMEM((width, sub_count * NI), f32),
+                pltpu.VMEM((width, (sub_count + 1) * NI), f32),
+                pltpu.VMEM((width, (sub_count + 1) * NI), f32),
                 pltpu.VMEM((3, n, case_count, width), f32),
                 pltpu.VMEM((5, case_count, NI), f32),
                 pltpu.VMEM((5, case_count, NI), f32),
@@ -548,8 +587,8 @@
                 pltpu.VMEM((1, n, 1, LANES), f32),
                 pltpu.VMEM((sub_count, case_count, unknowns), f32),
                 pltpu.SemaphoreType.DMA((10,)),
-                pltpu.SemaphoreType.DMA((5,)),
-                pltpu.SemaphoreType.DMA((5,)),
+                pltpu.SemaphoreType.DMA((4,)),
+                pltpu.SemaphoreType.DMA((4,)),
                 pltpu.SemaphoreType.DMA((8,)),
                 pltpu.SemaphoreType.DMA((8,)),
                 pltpu.SemaphoreType.DMA((5,)),

time: 55.7 us -> 50.7 us (0.910)
  Pallas kernels: 54.9 us -> 49.9 us
    pallas_call x1, Pallas kernels: 53.4 us -> 48.4 us  [shards(): pl.pallas_call(functools.partial(kernel, n, groups, inner), out_shape=res...]
where the time goes in v1:
time: 50.7 us; the launch traced here: 50.5 us
  Pallas kernels  49.9 us (98%)
  between operations  0.64 us (1%)
    pallas_call x1, Pallas kernels, shards(): pl.pallas_call(functools.partial(kernel, n, groups, inner), out_shape=res...  48.4 us
    pallas_call x1, Pallas kernels, shards(): pl.pallas_call(hand_over, out_shape=results, in_specs=[vmem] * 5, out_spe...  1.46 us

profile of v1, /device:TPU:0, one launch (start us, length us, event | category | flops | bytes accessed | tf_op | source)
XLA Modules:
  0.0 50.5 jit_solution(16132498802257266216)
XLA Ops:
  0.6 48.4 %shard_map.137 = (f32[8,2,512]{2,1,0:T(2,128)}, f32[8,2,512]{2,1,0:T(2,128)}, f32[8,256]{1,0:T(8,128)}, f32[8,8]{1,0:T(8,128)}, f32[8,1024]{1,0:T(8,128)}) custom-call(s32[32]{0:T(128)} %owner_hbm.1, f32[2,512,512]{2,1,0:T(8,128)} %rr_hbm.1, f32[2,64,512]{2,1,0:T(8,128)} %modes_hbm.1, f32[64,2048]{1,0:T(8,128)} %coarse_hbm.1, f32[1024,256]{1,0:T(8,128)} %basis_hbm.1, ...), custom_call_target="tpu_custom_call" | custom-call | tf_op jit(solution)/shard_map/pallas_call | solution.py:552
  49.0 1.5 %shard_map.138 = (f32[8,2,512]{2,1,0:T(2,128)}, f32[8,2,512]{2,1,0:T(2,128)}, f32[8,256]{1,0:T(8,128)}, f32[8,8]{1,0:T(8,128)}, f32[8,1024]{1,0:T(8,128)}) custom-call(f32[8,2,512]{2,1,0:T(2,128)} %get-tuple-element.15.refs_0_, f32[8,2,512]{2,1,0:T(2,128)} %get-tuple-element.16.refs_1_, f32[8,256]{1,0:T(8,128)} %get-tuple-element.17.refs_2_, ...), custom_call_target="tpu_custom_call" | custom-call | tf_op jit(solution)/shard_map/pallas_call | solution.py:610

commit v2 on v1

--- a/solution.py
+++ b/solution.py
@@ -33,29 +33,23 @@
 
 def split(x):
     first = x.astype(jnp.bfloat16)
-    rest = x - first.astype(jnp.float32)
-    second = rest.astype(jnp.bfloat16)
-    return first, second, (rest - second.astype(jnp.float32)).astype(jnp.bfloat16)
-
-
-def keep_split(parts, matrix):
-    for at, part in enumerate(split(matrix)):
-        parts[at] = part
+    return first, (x - first.astype(jnp.float32)).astype(jnp.bfloat16)
+
+
+def keep_split(parts, matrix, at=0):
+    for which, part in enumerate(split(matrix)):
+        parts[which, at : at + matrix.shape[0]] = part
 
 
 def split_dot(x, parts, contracted):
-    first, second, third = split(x)
-    stacked = jnp.concatenate([first, second, third, jnp.zeros_like(first)], axis=0)
+    first, second = split(x)
     rows = x.shape[0]
 
     def product(a, b):
         return lax.dot_general(a, b, (((1,), (contracted,)), ((), ())), preferred_element_type=jnp.float32)
 
-    large = product(stacked, parts[0])
-    middle = product(stacked[: 2 * rows], parts[1])
-    small = product(stacked[: 2 * rows], parts[2])
-    correction = large[2 * rows : 3 * rows] + middle[rows : 2 * rows] + small[:rows]
-    return large[:rows] + (large[rows : 2 * rows] + middle[:rows] + correction)
+    large = product(jnp.concatenate([first, second], axis=0), parts[0])
+    return large[:rows] + (large[rows:] + product(first, parts[1]))
 
 
 def hand_over(*refs):
@@ -91,8 +85,11 @@
     acc_now,
     load_next,
     coarse_parts,
-    forward_parts,
+    early_parts,
+    step_parts,
+    known_parts,
     backward_parts,
+    corner_parts,
     basis_parts,
     rr,
     modes,
@@ -103,6 +100,8 @@
     corner,
     forward,
     backward,
+    inward,
+    outgo,
     gathered,
     edge,
     edge_out,
@@ -224,18 +223,27 @@
     gathered[0, me] = placed(nt(jnp.concatenate(sides, axis=1), corner[...]))
 
     pl.semaphore_wait(barrier, n - 1)
+    next_modes = [
+        remote(modes.at[k, :, pl.ds(start, NI)], modes_next.at[at], const_send.at[at], const_recv.at[at], earlier)
+        for at, (k, start) in enumerate(((0, 0), (0, unknowns - NI), (1, 0)))
+    ]
+    halos = next_modes + [
+        remote(modes.at[1, :, pl.ds(unknowns - NI, NI)], modes_prev, const_send.at[3], const_recv.at[3], following)
+    ]
     broadcast(gathered, 0, 0)
-
+    for copy in halos:
+        copy.start()
     load_coarse.wait()
-    halos = [
+    coarse_near = [
         remote(
-            coarse.at[pl.ds(NC, NC)], coarse.at[pl.ds(3 * NC, NC)], const_send.at[0], const_recv.at[0], following
-        ),
-        remote(modes.at[1, :, pl.ds(unknowns - NI, NI)], modes_prev, const_send.at[1], const_recv.at[1], following),
-        remote(modes.at[0, :, pl.ds(0, NI)], modes_next, const_send.at[2], const_recv.at[2], earlier),
-        remote(coarse.at[pl.ds(0, NC)], coarse.at[pl.ds(2 * NC, NC)], const_send.at[3], const_recv.at[3], partner),
+            coarse.at[pl.ds(k * NC, NC)], coarse.at[pl.ds(slot * NC, NC)], const_send.at[4 + k], const_recv.at[4 + k], partner
+        )
+        for k, slot in ((0, 2), (1, 4))
     ]
-    for copy in halos:
+    coarse_far = remote(
+        coarse.at[pl.ds(NC, NC)], coarse.at[pl.ds(3 * NC, NC)], const_send.at[6], const_recv.at[6], following
+    )
+    for copy in coarse_near + [coarse_far]:
         copy.start()
 
     load_rr.wait()
@@ -249,6 +257,8 @@
 
     edges = []
     met = facing_edge(local[0][:, :NI], local[1][:, unknowns - NI :], 0)
+    middle_known = local[0][:, unknowns - NI :] - local[1][:, :NI]
+    met_middle = facing_edge(middle_known, middle_known, 5)
 
     load_owner.wait()
 
@@ -260,11 +270,53 @@
         return carry
 
     lax.fori_loop(0, n, find, 0)
+    keep_split(corner_parts, corner[...])
+    keep_split(coarse_parts, coarse[0:rows])
+    for copy in coarse_near:
+        copy.wait_recv()
+    keep_split(coarse_parts, coarse[2 * NC : 3 * NC], 2 * NC)
+    keep_split(coarse_parts, coarse[4 * NC :], 3 * NC)
     for copy in halos:
         copy.wait_recv()
     first0, last0 = modes[0, :, :NI], modes[0, :, unknowns - NI :]
     first1, last1 = modes[1, :, :NI], modes[1, :, unknowns - NI :]
-    before, after = modes_prev[...], modes_next[...]
+    before, after, after_last, after_first1 = modes_prev[...], modes_next[0], modes_next[1], modes_next[2]
+    jump = {
+        (-1, -2): before[:NC],
+        (-1, -1): before[NC:] - first0[:NC],
+        (-1, 0): -first0[NC:],
+        (0, -1): last0[:NC],
+        (0, 0): last0[NC:] - first1[:NC],
+        (0, 1): -first1[NC:],
+        (1, 0): last1[:NC],
+        (1, 1): last1[NC:] - after[:NC],
+        (1, 2): -after[NC:],
+        (2, 1): after_last[:NC],
+        (2, 2): after_last[NC:] - after_first1[:NC],
+        (2, 3): -after_first1[NC:],
+    }
+    for row, at_even, at_odd in ((0, 0, 0), (1, 1, 1), (2, 2, -2), (3, 3, -1)):
+        for i in range(-1, 3):
+            for target, (one, two) in ((inward, (at_even, at_odd)), (outgo, (at_odd, at_even))):
+                even_block, odd_block = jump.get((i, one), 0.0), jump.get((i, two), 0.0)
+                target[row * NC : (row + 1) * NC, (i + 1) * NI : (i + 2) * NI] = jnp.broadcast_to(
+                    even_block if one == two else jnp.where(odd, odd_block, even_block), (NC, NI)
+                )
+    nothing = jnp.zeros((2 * NC, NI), jnp.float32)
+    leaving = jnp.where(odd, last1, jnp.concatenate([-first0[NC:], nothing[:NC]], axis=0))
+    added = jnp.where(odd, jnp.concatenate([nothing[:NC], -after[:NC]], axis=0), 0.0)
+    keep_split(
+        early_parts,
+        jnp.concatenate(
+            [
+                nt(inward[...], outgo[...]),
+                jnp.concatenate([leaving, nothing], axis=0),
+                jnp.concatenate([added, nothing], axis=0),
+            ],
+            axis=1,
+        ),
+    )
+    keep_split(known_parts, outgo[...])
     forward[...] = jnp.zeros_like(forward)
     forward[0:NC, 0:NI] = -first0[NC:]
     forward[0:NC, NI : 2 * NI] = last0[NC:] - first1[:NC]
@@ -284,18 +336,20 @@
     backward[3 * NC :, 0:NI] = jnp.where(odd, 0.0, before[NC:] - first0[:NC])
     backward[3 * NC :, NI : 2 * NI] = last0[:NC]
 
-    keep_split(forward_parts, forward[...])
+    keep_split(step_parts, jnp.concatenate([forward[...], nt(forward[...], backward[...])], axis=1))
     keep_split(backward_parts, backward[...])
-    keep_split(coarse_parts, coarse[...])
-
-    def coarse_solve(at):
+
+    def assemble(at):
         all_but_one(gathered, at, wide_recv.at[at]).wait()
         assembled = []
         for j in range(n // 2):
             low = jnp.where(lane < 64, gathered[at, 2 * j], gathered[at, (2 * j + 2) % n])
-            high = jnp.where(lane >= 32, gathered[at, 2 * j + 1], gathered[at, (2 * j - 1) % n])
+            high = jnp.where(lane >= (64 if at == 1 else 32), gathered[at, 2 * j + 1], gathered[at, (2 * j - 1) % n])
             assembled.append(low + high)
-        return split_dot(jnp.concatenate(assembled, axis=1), coarse_parts, 1)
+        return jnp.concatenate(assembled, axis=1)
+
+    def coarse_solve(at):
+        return split_dot(assemble(at), coarse_parts, 1)
 
     def jumps(fields, across):
         first, second = fields
@@ -305,41 +359,64 @@
 
     per_piece = unknowns // n
     width = sub_count * per_piece
+    per_tile = LANES // width
+    spot = lax.rem(me, per_tile)
 
     def piece_part(fields, which, p):
         block = p * per_piece // LANES
         inside = p * per_piece % LANES
+        start = lax.rem(spot + which, per_tile) * width
         part = jnp.zeros((8, LANES), jnp.float32)
         for k in range(sub_count):
-            target = which * width + k * per_piece
+            target = start + k * per_piece
             rolled = pltpu.roll(
-                fields[k][:, block * LANES : (block + 1) * LANES], (target - inside) % LANES, 1
+                fields[k][:, block * LANES : (block + 1) * LANES], lax.rem(target + LANES - inside, LANES), 1
             )
             part = jnp.where((lane >= target) & (lane < target + per_piece), rolled, part)
         return part
 
-    solved = coarse_solve(0)
-    met.wait_recv()
-    vector0 = jumps(local, edge[0]) + split_dot(solved, forward_parts, 0)
-
-    def start_image(vector, at):
-        gathered[at, me] = placed(split_dot(vector, backward_parts, 1))
-        broadcast(gathered, at, at)
+    def outer_half(vector, at):
         slot = 2 * at - 1
-        edge_out[slot] = jnp.where(odd, vector[:, 2 * NI :], vector[:, :NI])
+        edge_out[slot] = vector
         copy = remote(edge_out.at[slot], edge.at[slot], edge_send.at[slot], edge_recv.at[slot], outward)
         copy.start()
         edges.append(copy)
+        return copy
+
+    def send_terms(terms, at):
+        gathered[at, me] = placed(terms)
+        broadcast(gathered, at, at)
+
+    def outermost(vector):
+        return jnp.where(odd, vector[:, 2 * NI : 3 * NI], vector[:, :NI])
+
+    def facing_field(vector, at):
         left, middle, right = vector[:, :NI], vector[:, NI : 2 * NI], vector[:, 2 * NI :]
         near = rr.at[jnp.where(odd, 0, 1)]
         facing = nn(jnp.where(odd, -left, -middle), near[:NI, :]) + nn(
             jnp.where(odd, middle, right), near[unknowns - NI :, :]
         )
-        return copy, facing_edge(facing[:, :NI], facing[:, unknowns - NI :], slot + 1), facing
-
-    def whole(vector, copy, at):
+        return facing_edge(facing[:, :NI], facing[:, unknowns - NI :], 2 * at), facing
+
+    met.wait_recv()
+    known = jumps(local, edge[0])
+    met_middle.wait_recv()
+    carried = split_dot(jnp.concatenate([known, jnp.where(odd, 0.0, edge[5])], axis=1), known_parts, 1)
+    assembled = assemble(0)
+    solved = split_dot(assembled, coarse_parts, 1)
+    early = split_dot(solved, early_parts, 0)
+    sent0 = outer_half(outermost(known) + early[:, LANES : LANES + NI], 1)
+    send_terms(carried + early[:, :LANES], 1)
+    extra = early[:, LANES + NI :]
+    coarse_far.wait_recv()
+    keep_split(coarse_parts, coarse[3 * NC : 4 * NC], 3 * NC)
+    solved = jnp.concatenate([solved[:, : 3 * NC], split_dot(assembled, coarse_parts.at[:, pl.ds(3 * NC, NC)], 1)], axis=1)
+    vector0 = known + split_dot(solved, step_parts, 0)[:, : 3 * NI]
+    met0, facing0 = facing_field(vector0, 1)
+
+    def whole(vector, copy, at, extra=0.0):
         copy.wait_recv()
-        other = edge[2 * at - 1]
+        other = edge[2 * at - 1] + extra
         return jnp.concatenate(
             [
                 vector[:, :NI] + jnp.where(odd, 0.0, other),
@@ -358,56 +435,64 @@
         inside = [jnp.where(odd, facing, outer_field), jnp.where(odd, outer_field, facing)]
         met.wait_recv()
         known = jumps(inside, edge[2 * at])
-        values = coarse_solve(at)
-        return inside, values, known + split_dot(values, forward_parts, 0)
+        carried = split_dot(known, backward_parts, 1)
+        return inside, known, carried, coarse_solve(at)
 
     def counted(vector):
         return jnp.concatenate([jnp.where(odd, 0.0, vector[:, :NI]), vector[:, NI:]], axis=1)
 
     def with_corners(inside, values):
-        return [
-            inside[k] + nn(values, corner[:, k * unknowns : (k + 1) * unknowns]) for k in range(sub_count)
-        ]
+        added = split_dot(values, corner_parts, 0)
+        return [inside[k] + added[:, k * unknowns : (k + 1) * unknowns] for k in range(sub_count)]
 
     def column(values):
         return jnp.sum(values, axis=1, keepdims=True)
 
-    sent0, met0, facing0 = start_image(vector0, 1)
     first_fields = with_corners(local, solved)
     for k in range(sub_count):
         green[k] = first_fields[k]
     for p in range(n):
         pieces[p] = piece_part(first_fields, 0, p)
-    full0 = whole(vector0, sent0, 1)
-    inside0, values0, vector1 = end_image(full0, met0, facing0, 1)
-
-    sent1, met1, facing1 = start_image(vector1, 2)
+    full0 = whole(vector0, sent0, 1, extra)
+    inside0, known, carried, values0 = end_image(full0, met0, facing0, 1)
+
+    step = split_dot(values0, step_parts, 0)
+    vector1 = known + step[:, : 3 * NI]
+    sent1 = outer_half(outermost(vector1), 2)
+    send_terms(carried + step[:, 3 * NI :], 2)
     norm_row = jnp.where(lane == sublane, column(full0 * counted(vector0)), 0.0) + jnp.where(
         lane == sublane + 8, column(full0 * counted(vector1)), 0.0
     )
     norms[0, me] = jnp.sum(norm_row, axis=0, keepdims=True)
     broadcast(norms, 0, 3)
+    met1, facing1 = facing_field(vector1, 2)
     fields0 = with_corners(inside0, values0)
     for p in range(n):
         pieces[p] = pieces[p] + piece_part(fields0, 1, p)
     load_basis.wait()
     keep_split(basis_parts, basis[...])
     full1 = whole(vector1, sent1, 2)
-    inside1, values1, vector2 = end_image(full1, met1, facing1, 2)
+    weighed0, weighed1 = [
+        split_dot(counted(full), step_parts.at[:, :, pl.ds(0, 3 * NI)], 1) for full in (full0, full1)
+    ]
+    inside1, known, carried, values1 = end_image(full1, met1, facing1, 2)
     fields1 = with_corners(inside1, values1)
 
     all_but_one(norms, 0, wide_recv.at[3]).wait()
     totals = jnp.broadcast_to(jnp.sum(norms[0], axis=0), (8, LANES))
-    norm0 = column(jnp.where(lane == sublane, totals, 0.0))
-    curve0 = column(jnp.where(lane == sublane + 8, totals, 0.0))
+    norm0, curve0 = [column(jnp.where(lane == sublane + 8 * which, totals, 0.0)) for which in range(2)]
     alpha0 = norm0 / curve0
-    residual = full0 - alpha0 * full1
-    residual_part = counted(vector0 - alpha0 * vector1)
-    residual_image = counted(vector1 - alpha0 * vector2)
+    residual = counted(full0 - alpha0 * full1)
+    free = lax.rem(spot + 3, per_tile) * width + per_piece
     extra = (
-        jnp.where(lane == 3 * width, column(residual * residual_part), 0.0)
-        + jnp.where(lane == 3 * width + 1, column(residual * residual_image), 0.0)
-        + jnp.where(lane == 3 * width + 2, column(residual * counted(vector1)), 0.0)
+        jnp.where(lane == free, column(residual * (vector0 - alpha0 * vector1)), 0.0)
+        + jnp.where(
+            lane == free + 1,
+            column(residual * (vector1 - alpha0 * known))
+            - alpha0 * column((weighed0 - alpha0 * weighed1) * values1),
+            0.0,
+        )
+        + jnp.where(lane == free + 2, column(residual * vector1), 0.0)
     )
     for p in range(n):
         pieces[p] = pieces[p] + piece_part(fields1, 2, p) + extra
@@ -420,32 +505,35 @@
     others(send_piece)
     incoming[0, me] = outgoing[me]
     all_but_one(incoming, 0, wide_recv.at[4]).wait()
-
-    sums = jnp.sum(incoming[0], axis=0)
-    norm1 = column(jnp.where(lane == 3 * width, sums, 0.0))
-    curve_rr = column(jnp.where(lane == 3 * width + 1, sums, 0.0))
-    curve_rp = column(jnp.where(lane == 3 * width + 2, sums, 0.0))
+    gathered_sums = jnp.zeros((8, LANES), jnp.float32)
+    for i in range(per_tile):
+        total = incoming[0, i]
+        for j in range(1, n // per_tile):
+            total = total + incoming[0, j * per_tile + i]
+        at = (i + 3) % per_tile * width + per_piece
+        gathered_sums = jnp.where((lane >= at) & (lane < at + 3), total, gathered_sums)
+    norm1, curve_rr, curve_rp = [
+        column(jnp.where(lax.rem(lane, width) == per_piece + which, gathered_sums, 0.0)) for which in range(3)
+    ]
     beta = norm1 / norm0
     curve1 = curve_rr + 2.0 * beta * curve_rp + beta * beta * curve0
     alpha1 = norm1 / curve1
     scale0 = alpha0 + alpha1 * (1.0 + beta)
     scale1 = -alpha1 * alpha0
 
-    factor = jnp.where(lane < width, 1.0, jnp.where(lane < 2 * width, -scale0, -scale1))
-    factor = jnp.where(lane < 3 * width, factor, 0.0)
-    per_tile = LANES // width
     snapshot_tiles = []
     for j in range(n // per_tile):
-        tile = jnp.zeros((8, LANES), jnp.float32)
-        for i in range(per_tile):
-            scaled = incoming[0, j * per_tile + i] * factor
-            total = scaled
-            for which in (1, 2):
-                total = total + pltpu.roll(scaled, LANES - which * width, 1)
-            if i:
-                total = pltpu.roll(total, i * width, 1)
-            tile = jnp.where((lane >= i * width) & (lane < (i + 1) * width), total, tile)
-        snapshot_tiles.append(tile)
+        total = jnp.zeros((8, LANES), jnp.float32)
+        for which, factor in enumerate((1.0, -scale0, -scale1)):
+            tile = incoming[0, j * per_tile]
+            for i in range(1, per_tile):
+                block = (i + which) % per_tile
+                inside = (lane >= block * width) & (lane < (block + 1) * width)
+                tile = jnp.where(inside, incoming[0, j * per_tile + i], tile)
+            if which:
+                tile = pltpu.roll(tile, LANES - which * width, 1)
+            total = total + factor * tile
+        snapshot_tiles.append(total)
     snapshots = jnp.concatenate(snapshot_tiles, axis=1)
     proj_parts[seat] = split_dot(snapshots, basis_parts, 0)
     for i in range(1, inner):
@@ -486,24 +574,28 @@
     broadcast(gram_parts, 0, 6)
     all_but_one(gram_parts, 0, wide_recv.at[6]).wait()
     gram_row = jnp.broadcast_to(jnp.sum(gram_parts[0], axis=0), (8, LANES))
-    work = gram_row
-    for i in range(1, 8):
-        work = jnp.where(sublane == i, pltpu.roll(gram_row, LANES - 8 * i, 1), work)
+    entry = {
+        (i, j): jnp.broadcast_to(gram_row[:, 8 * i + j : 8 * i + j + 1], (8, LANES)) for i in range(8) for j in range(i + 1)
+    }
+    row_at = lax.broadcasted_iota(jnp.int32, remainder.shape, 0)
+    factor = jnp.zeros((8, LANES), jnp.float32)
     for j in range(8):
-        inverse_root = lax.rsqrt(work[j : j + 1, j : j + 1])
-        pivot = work[j : j + 1, :] * inverse_root
-        below = work[:, j : j + 1] * inverse_root
-        pivot_rows = remainder[j : j + 1, :] * inverse_root
-        work = jnp.where(sublane == j, pivot, jnp.where(sublane > j, work - below * pivot, work))
-        row_at = lax.broadcasted_iota(jnp.int32, remainder.shape, 0)
-        remainder = jnp.where(
-            row_at == j, pivot_rows, jnp.where(row_at > j, remainder - below * pivot_rows, remainder)
-        )
+        inverse_root = lax.rsqrt(entry[j, j])
+        lower = {i: entry[i, j] * inverse_root for i in range(j, 8)}
+        below = jnp.zeros((8, LANES), jnp.float32)
+        for i in range(j, 8):
+            factor = jnp.where((sublane == j) & (lane == i), lower[i], factor)
+            for k in range(j + 1, i + 1):
+                entry[i, k] = entry[i, k] - lower[i] * lower[k]
+            if i > j:
+                below = jnp.where(sublane == i, lower[i], below)
+        pivot_rows = remainder[j : j + 1, :] * inverse_root[0:1, 0:1]
+        remainder = jnp.where(row_at == j, pivot_rows, remainder - below[:, 0:1] * pivot_rows)
     scale_rows = math.sqrt(snapshots.shape[1] * n)
-    r_out[...] = jnp.where(lane >= sublane, work, 0.0)[:, :8] * (1.0 / scale_rows)
+    r_out[...] = factor[:, :8] * (1.0 / scale_rows)
     cols_out[...] = remainder * scale_rows
 
-    for copy in halos + edges:
+    for copy in halos + coarse_near + [coarse_far] + edges:
         copy.wait_send()
     for at in range(3):
         all_but_one(gathered, at, wide_send.at[at]).wait()
@@ -549,9 +641,10 @@
             jax.ShapeDtypeStruct((case_count, case_count), f32),
             jax.ShapeDtypeStruct((case_count, local_rows), f32),
         )
+        kept = tuple(pltpu.VMEM(result.shape, f32) for result in results)
         computed = pl.pallas_call(
             functools.partial(kernel, n, groups, inner),
-            out_shape=results,
+            out_shape=kept,
             in_specs=[anywhere] * 10,
             out_specs=(vmem,) * 5,
             scratch_shapes=[
@@ -562,22 +655,27 @@
                 pltpu.VMEM(vel_now.shape, f32),
                 pltpu.VMEM(acc_now.shape, f32),
                 pltpu.VMEM(load_next.shape, f32),
-                pltpu.VMEM((3, width, coarse_inverse.shape[1]), jnp.bfloat16),
-                pltpu.VMEM((3, width, (sub_count + 1) * NI), jnp.bfloat16),
-                pltpu.VMEM((3, width, (sub_count + 1) * NI), jnp.bfloat16),
-                pltpu.VMEM((3,) + basis_rows.shape, jnp.bfloat16),
+                pltpu.VMEM((2, width, coarse_inverse.shape[1]), jnp.bfloat16),
+                pltpu.VMEM((2, width, width + 2 * NI), jnp.bfloat16),
+                pltpu.VMEM((2, width, (sub_count + 1) * NI + width), jnp.bfloat16),
+                pltpu.VMEM((2, width, (sub_count + 2) * NI), jnp.bfloat16),
+                pltpu.VMEM((2, width, (sub_count + 1) * NI), jnp.bfloat16),
+                pltpu.VMEM((2, width, sub_count * unknowns), jnp.bfloat16),
+                pltpu.VMEM((2,) + basis_rows.shape, jnp.bfloat16),
                 pltpu.VMEM(rr_inverse.shape, f32),
                 pltpu.VMEM(corner_modes.shape, f32),
-                pltpu.VMEM((width, coarse_inverse.shape[1]), f32),
+                pltpu.VMEM((width + NC, coarse_inverse.shape[1]), f32),
                 pltpu.VMEM(basis_rows.shape, f32),
-                pltpu.VMEM((2 * NC, NI), f32),
+                pltpu.VMEM((3, 2 * NC, NI), f32),
                 pltpu.VMEM((2 * NC, NI), f32),
                 pltpu.VMEM((width, sub_count * unknowns), f32),
                 pltpu.VMEM((width, (sub_count + 1) * NI), f32),
                 pltpu.VMEM((width, (sub_count + 1) * NI), f32),
+                pltpu.VMEM((width, (sub_count + 2) * NI), f32),
+                pltpu.VMEM((width, (sub_count + 2) * NI), f32),
                 pltpu.VMEM((3, n, case_count, width), f32),
-                pltpu.VMEM((5, case_count, NI), f32),
-                pltpu.VMEM((5, case_count, NI), f32),
+                pltpu.VMEM((6, case_count, NI), f32),
+                pltpu.VMEM((6, case_count, NI), f32),
                 pltpu.VMEM((1, n, 1, LANES), f32),
                 pltpu.VMEM((n, case_count, LANES), f32),
                 pltpu.VMEM((n, case_count, LANES), f32),
@@ -587,12 +685,12 @@
                 pltpu.VMEM((1, n, 1, LANES), f32),
                 pltpu.VMEM((sub_count, case_count, unknowns), f32),
                 pltpu.SemaphoreType.DMA((10,)),
-                pltpu.SemaphoreType.DMA((4,)),
-                pltpu.SemaphoreType.DMA((4,)),
+                pltpu.SemaphoreType.DMA((7,)),
+                pltpu.SemaphoreType.DMA((7,)),
                 pltpu.SemaphoreType.DMA((8,)),
                 pltpu.SemaphoreType.DMA((8,)),
-                pltpu.SemaphoreType.DMA((5,)),
-                pltpu.SemaphoreType.DMA((5,)),
+                pltpu.SemaphoreType.DMA((6,)),
+                pltpu.SemaphoreType.DMA((6,)),
             ],
             compiler_params=pltpu.CompilerParams(collective_id=0, has_side_effects=True),
         )(
@@ -608,7 +706,11 @@
             load_next,
         )
         disp, vel, proj, r_factor, columns = pl.pallas_call(
-            hand_over, out_shape=results, in_specs=[vmem] * 5, out_specs=(vmem,) * 5
+            hand_over,
+            out_shape=results,
+            in_specs=[vmem] * 5,
+            out_specs=(vmem,) * 5,
+            compiler_params=pltpu.CompilerParams(vmem_limit_bytes=4 * 1024 * 1024),
         )(*computed)
         return disp, vel, proj.T, r_factor, columns
 

time: 50.7 us -> 46.6 us (0.919)
  Pallas kernels: 49.9 us -> 45.8 us
    pallas_call x1, Pallas kernels: 48.4 us -> 45.1 us  [shards(): pl.pallas_call(functools.partial(kernel, n, groups, inner), out_shape=kep...]
    pallas_call x1, Pallas kernels: 1.46 us -> 0.65 us  [shards(): pl.pallas_call(hand_over, out_shape=results, in_specs=[vmem] * 5, out_spe...]
where the time goes in v2:
time: 46.6 us; the launch traced here: 46.4 us
  Pallas kernels  45.8 us (98%)
  between operations  0.64 us (1%)
    pallas_call x1, Pallas kernels, shards(): pl.pallas_call(functools.partial(kernel, n, groups, inner), out_shape=kep...  45.1 us

profile of v2, /device:TPU:0, one launch (start us, length us, event | category | flops | bytes accessed | tf_op | source)
XLA Modules:
  0.0 46.4 jit_solution(65949706499894453)
XLA Ops:
  0.6 45.1 %shard_map.137 = (f32[8,2,512]{2,1,0:T(2,128)S(1)}, f32[8,2,512]{2,1,0:T(2,128)S(1)}, f32[8,256]{1,0:T(8,128)S(1)}, f32[8,8]{1,0:T(8,128)S(1)}, f32[8,1024]{1,0:T(8,128)S(1)}) custom-call(s32[32]{0:T(128)} %owner_hbm.1, f32[2,512,512]{2,1,0:T(8,128)} %rr_hbm.1, f32[2,64,512]{2,1,0:T(8,128)} %modes_hbm.1, f32[64,2048]{1,0:T(8,128)} %coarse_hbm.1, ...), custom_call_target="tpu_custom_call" | custom-call | tf_op jit(solution)/shard_map/pallas_call | solution.py:645
  45.8 0.7 %shard_map.138 = (f32[8,2,512]{2,1,0:T(2,128)}, f32[8,2,512]{2,1,0:T(2,128)}, f32[8,256]{1,0:T(8,128)}, f32[8,8]{1,0:T(8,128)}, f32[8,1024]{1,0:T(8,128)}) custom-call(f32[8,2,512]{2,1,0:T(2,128)S(1)} %get-tuple-element.15.refs_0_, f32[8,2,512]{2,1,0:T(2,128)S(1)} %get-tuple-element.16.refs_1_, f32[8,256]{1,0:T(8,128)S(1)} %get-tuple-element.17.refs_2_, ...), custom_call_target="tpu_custom_call" | custom-call | tf_op jit(solution)/shard_map/pallas_call | solution.py:708

commit v3 on v2

--- a/solution.py
+++ b/solution.py
@@ -39,6 +39,11 @@
 def keep_split(parts, matrix, at=0):
     for which, part in enumerate(split(matrix)):
         parts[which, at : at + matrix.shape[0]] = part
+
+
+def keep_columns(parts, matrix, at=0):
+    for which, part in enumerate(split(matrix)):
+        parts[which, :, at : at + matrix.shape[1]] = part
 
 
 def split_dot(x, parts, contracted):
@@ -91,6 +96,7 @@
     backward_parts,
     corner_parts,
     basis_parts,
+    basis_across,
     rr,
     modes,
     coarse,
@@ -100,8 +106,6 @@
     corner,
     forward,
     backward,
-    inward,
-    outgo,
     gathered,
     edge,
     edge_out,
@@ -271,16 +275,15 @@
 
     lax.fori_loop(0, n, find, 0)
     keep_split(corner_parts, corner[...])
-    keep_split(coarse_parts, coarse[0:rows])
+
     for copy in coarse_near:
         copy.wait_recv()
-    keep_split(coarse_parts, coarse[2 * NC : 3 * NC], 2 * NC)
-    keep_split(coarse_parts, coarse[4 * NC :], 3 * NC)
-    for copy in halos:
-        copy.wait_recv()
+    keep_columns(coarse_parts, jnp.concatenate([coarse[: 3 * NC], coarse[4 * NC :]], axis=0).T)
+    halos[3].wait_recv()
     first0, last0 = modes[0, :, :NI], modes[0, :, unknowns - NI :]
     first1, last1 = modes[1, :, :NI], modes[1, :, unknowns - NI :]
-    before, after, after_last, after_first1 = modes_prev[...], modes_next[0], modes_next[1], modes_next[2]
+    before = modes_prev[...]
+    empty = jnp.zeros((2 * NC, NI), jnp.float32)
     jump = {
         (-1, -2): before[:NC],
         (-1, -1): before[NC:] - first0[:NC],
@@ -289,34 +292,103 @@
         (0, 0): last0[NC:] - first1[:NC],
         (0, 1): -first1[NC:],
         (1, 0): last1[:NC],
-        (1, 1): last1[NC:] - after[:NC],
-        (1, 2): -after[NC:],
-        (2, 1): after_last[:NC],
-        (2, 2): after_last[NC:] - after_first1[:NC],
-        (2, 3): -after_first1[NC:],
     }
-    for row, at_even, at_odd in ((0, 0, 0), (1, 1, 1), (2, 2, -2), (3, 3, -1)):
-        for i in range(-1, 3):
-            for target, (one, two) in ((inward, (at_even, at_odd)), (outgo, (at_odd, at_even))):
-                even_block, odd_block = jump.get((i, one), 0.0), jump.get((i, two), 0.0)
-                target[row * NC : (row + 1) * NC, (i + 1) * NI : (i + 2) * NI] = jnp.broadcast_to(
-                    even_block if one == two else jnp.where(odd, odd_block, even_block), (NC, NI)
-                )
-    nothing = jnp.zeros((2 * NC, NI), jnp.float32)
-    leaving = jnp.where(odd, last1, jnp.concatenate([-first0[NC:], nothing[:NC]], axis=0))
-    added = jnp.where(odd, jnp.concatenate([nothing[:NC], -after[:NC]], axis=0), 0.0)
-    keep_split(
-        early_parts,
-        jnp.concatenate(
-            [
-                nt(inward[...], outgo[...]),
-                jnp.concatenate([leaving, nothing], axis=0),
-                jnp.concatenate([added, nothing], axis=0),
-            ],
-            axis=1,
-        ),
+
+    def fill_columns(i):
+        for parts, swap in ((early_parts, False), (known_parts, True)):
+            blocks = []
+            for ends in ((0, 0), (1, 1), (2, -2), (3, -1)):
+                at_even, at_odd = [jump.get((i, end), empty[:NC]) for end in (ends[::-1] if swap else ends)]
+                blocks.append(at_even if ends[0] == ends[1] else jnp.where(odd, at_odd, at_even))
+            keep_columns(parts, jnp.concatenate(blocks, axis=0), (i + 1) * NI)
+
+    fill_columns(-1)
+    fill_columns(0)
+    leaving = jnp.where(odd, last1, jnp.concatenate([-first0[NC:], empty[:NC]], axis=0))
+    keep_columns(early_parts, jnp.concatenate([leaving, empty], axis=0), 4 * NI)
+    def assemble(at):
+        all_but_one(gathered, at, wide_recv.at[at]).wait()
+        assembled = []
+        for j in range(n // 2):
+            low = jnp.where(lane < 64, gathered[at, 2 * j], gathered[at, (2 * j + 2) % n])
+            high = jnp.where(lane >= (64 if at == 1 else 32), gathered[at, 2 * j + 1], gathered[at, (2 * j - 1) % n])
+            assembled.append(low + high)
+        return jnp.concatenate(assembled, axis=1)
+
+    def coarse_solve(at):
+        return split_dot(assemble(at), coarse_parts, 0)
+
+    def jumps(fields, across):
+        first, second = fields
+        left = jnp.where(odd, across, 0.0) - first[:, :NI]
+        right = second[:, unknowns - NI :] - jnp.where(odd, 0.0, across)
+        return jnp.concatenate([left, first[:, unknowns - NI :] - second[:, :NI], right], axis=1)
+
+    per_piece = unknowns // n
+    width = sub_count * per_piece
+    per_tile = LANES // width
+    spot = lax.rem(me, per_tile)
+
+    def piece_part(fields, which, p):
+        block = p * per_piece // LANES
+        inside = p * per_piece % LANES
+        start = lax.rem(spot + which, per_tile) * width
+        part = jnp.zeros((8, LANES), jnp.float32)
+        for k in range(sub_count):
+            target = start + k * per_piece
+            rolled = pltpu.roll(
+                fields[k][:, block * LANES : (block + 1) * LANES], lax.rem(target + LANES - inside, LANES), 1
+            )
+            part = jnp.where((lane >= target) & (lane < target + per_piece), rolled, part)
+        return part
+
+    def outer_half(vector, at):
+        slot = 2 * at - 1
+        edge_out[slot] = vector
+        copy = remote(edge_out.at[slot], edge.at[slot], edge_send.at[slot], edge_recv.at[slot], outward)
+        copy.start()
+        edges.append(copy)
+        return copy
+
+    def send_terms(terms, at):
+        gathered[at, me] = placed(terms)
+        broadcast(gathered, at, at)
+
+    def outermost(vector):
+        return jnp.where(odd, vector[:, 2 * NI : 3 * NI], vector[:, :NI])
+
+    def facing_field(vector, at):
+        left, middle, right = vector[:, :NI], vector[:, NI : 2 * NI], vector[:, 2 * NI :]
+        near = rr.at[jnp.where(odd, 0, 1)]
+        facing = nn(jnp.where(odd, -left, -middle), near[:NI, :]) + nn(
+            jnp.where(odd, middle, right), near[unknowns - NI :, :]
+        )
+        return facing_edge(facing[:, :NI], facing[:, unknowns - NI :], 2 * at), facing
+
+    met.wait_recv()
+    known = jumps(local, edge[0])
+    met_middle.wait_recv()
+    known_wide = jnp.concatenate([known, jnp.where(odd, 0.0, edge[5])], axis=1)
+    assembled = assemble(0)
+    solved = split_dot(assembled, coarse_parts, 0)
+    for copy in next_modes:
+        copy.wait_recv()
+    after, after_last, after_first1 = modes_next[0], modes_next[1], modes_next[2]
+    jump.update(
+        {
+            (1, 1): last1[NC:] - after[:NC],
+            (1, 2): -after[NC:],
+            (2, 1): after_last[:NC],
+            (2, 2): after_last[NC:] - after_first1[:NC],
+            (2, 3): -after_first1[NC:],
+        }
     )
-    keep_split(known_parts, outgo[...])
+    fill_columns(1)
+    fill_columns(2)
+    keep_columns(early_parts, jnp.concatenate([empty[:NC], jnp.where(odd, -after[:NC], 0.0), empty], axis=0), 5 * NI)
+    early = split_dot(solved, early_parts, 0)
+    sent0 = outer_half(outermost(known) + early[:, 4 * NI : 5 * NI], 1)
+    send_terms(split_dot(known_wide + early[:, : 4 * NI], known_parts, 1), 1)
     forward[...] = jnp.zeros_like(forward)
     forward[0:NC, 0:NI] = -first0[NC:]
     forward[0:NC, NI : 2 * NI] = last0[NC:] - first1[:NC]
@@ -338,79 +410,10 @@
 
     keep_split(step_parts, jnp.concatenate([forward[...], nt(forward[...], backward[...])], axis=1))
     keep_split(backward_parts, backward[...])
-
-    def assemble(at):
-        all_but_one(gathered, at, wide_recv.at[at]).wait()
-        assembled = []
-        for j in range(n // 2):
-            low = jnp.where(lane < 64, gathered[at, 2 * j], gathered[at, (2 * j + 2) % n])
-            high = jnp.where(lane >= (64 if at == 1 else 32), gathered[at, 2 * j + 1], gathered[at, (2 * j - 1) % n])
-            assembled.append(low + high)
-        return jnp.concatenate(assembled, axis=1)
-
-    def coarse_solve(at):
-        return split_dot(assemble(at), coarse_parts, 1)
-
-    def jumps(fields, across):
-        first, second = fields
-        left = jnp.where(odd, across, 0.0) - first[:, :NI]
-        right = second[:, unknowns - NI :] - jnp.where(odd, 0.0, across)
-        return jnp.concatenate([left, first[:, unknowns - NI :] - second[:, :NI], right], axis=1)
-
-    per_piece = unknowns // n
-    width = sub_count * per_piece
-    per_tile = LANES // width
-    spot = lax.rem(me, per_tile)
-
-    def piece_part(fields, which, p):
-        block = p * per_piece // LANES
-        inside = p * per_piece % LANES
-        start = lax.rem(spot + which, per_tile) * width
-        part = jnp.zeros((8, LANES), jnp.float32)
-        for k in range(sub_count):
-            target = start + k * per_piece
-            rolled = pltpu.roll(
-                fields[k][:, block * LANES : (block + 1) * LANES], lax.rem(target + LANES - inside, LANES), 1
-            )
-            part = jnp.where((lane >= target) & (lane < target + per_piece), rolled, part)
-        return part
-
-    def outer_half(vector, at):
-        slot = 2 * at - 1
-        edge_out[slot] = vector
-        copy = remote(edge_out.at[slot], edge.at[slot], edge_send.at[slot], edge_recv.at[slot], outward)
-        copy.start()
-        edges.append(copy)
-        return copy
-
-    def send_terms(terms, at):
-        gathered[at, me] = placed(terms)
-        broadcast(gathered, at, at)
-
-    def outermost(vector):
-        return jnp.where(odd, vector[:, 2 * NI : 3 * NI], vector[:, :NI])
-
-    def facing_field(vector, at):
-        left, middle, right = vector[:, :NI], vector[:, NI : 2 * NI], vector[:, 2 * NI :]
-        near = rr.at[jnp.where(odd, 0, 1)]
-        facing = nn(jnp.where(odd, -left, -middle), near[:NI, :]) + nn(
-            jnp.where(odd, middle, right), near[unknowns - NI :, :]
-        )
-        return facing_edge(facing[:, :NI], facing[:, unknowns - NI :], 2 * at), facing
-
-    met.wait_recv()
-    known = jumps(local, edge[0])
-    met_middle.wait_recv()
-    carried = split_dot(jnp.concatenate([known, jnp.where(odd, 0.0, edge[5])], axis=1), known_parts, 1)
-    assembled = assemble(0)
-    solved = split_dot(assembled, coarse_parts, 1)
-    early = split_dot(solved, early_parts, 0)
-    sent0 = outer_half(outermost(known) + early[:, LANES : LANES + NI], 1)
-    send_terms(carried + early[:, :LANES], 1)
-    extra = early[:, LANES + NI :]
+    extra = early[:, 5 * NI :]
     coarse_far.wait_recv()
-    keep_split(coarse_parts, coarse[3 * NC : 4 * NC], 3 * NC)
-    solved = jnp.concatenate([solved[:, : 3 * NC], split_dot(assembled, coarse_parts.at[:, pl.ds(3 * NC, NC)], 1)], axis=1)
+    keep_columns(coarse_parts, coarse[: 4 * NC].T)
+    solved = jnp.concatenate([solved[:, : 3 * NC], split_dot(assembled, coarse_parts, 0)[:, 3 * NC :]], axis=1)
     vector0 = known + split_dot(solved, step_parts, 0)[:, : 3 * NI]
     met0, facing0 = facing_field(vector0, 1)
 
@@ -504,6 +507,7 @@
 
     others(send_piece)
     incoming[0, me] = outgoing[me]
+    keep_columns(basis_across, basis[...].T)
     all_but_one(incoming, 0, wide_recv.at[4]).wait()
     gathered_sums = jnp.zeros((8, LANES), jnp.float32)
     for i in range(per_tile):
@@ -540,6 +544,13 @@
         rank = plane * inner + lax.rem(seat + i, inner)
         remote(proj_parts.at[seat], proj_parts.at[seat], wide_send.at[5], wide_recv.at[5], rank).start()
 
+    for copy in halos + coarse_near + [coarse_far] + edges:
+        copy.wait_send()
+    for at in range(3):
+        all_but_one(gathered, at, wide_send.at[at]).wait()
+    all_but_one(norms, 0, wide_send.at[3]).wait()
+    all_but_one(incoming, 0, wide_send.at[4]).wait()
+
     for k in range(sub_count):
         carried = green[k] - scale0 * fields0[k] - scale1 * fields1[k]
         now, vel, acc = disp_now[:, k, :], vel_now[:, k, :], acc_now[:, k, :]
@@ -563,7 +574,7 @@
     ).wait()
     projection = jnp.sum(proj_sums[...], axis=0)
     proj_out[...] = projection
-    remainder = snapshots - split_dot(projection, basis_parts, 1)
+    remainder = snapshots - split_dot(projection, basis_across, 0)
     gram_row = jnp.zeros((8, LANES), jnp.float32)
     for shift in range(5):
         product = remainder * pltpu.roll(remainder, shift, 0)
@@ -572,6 +583,12 @@
         gram_row = jnp.where(here, column(product), gram_row)
     gram_parts[0, me] = jnp.sum(gram_row, axis=0, keepdims=True)
     broadcast(gram_parts, 0, 6)
+    pltpu.make_async_copy(
+        proj_parts.at[pl.ds(0, inner - 1)], proj_parts.at[pl.ds(0, inner - 1)], wide_send.at[5]
+    ).wait()
+    pltpu.make_async_copy(
+        proj_sums.at[pl.ds(0, outer - 1)], proj_sums.at[pl.ds(0, outer - 1)], wide_send.at[7]
+    ).wait()
     all_but_one(gram_parts, 0, wide_recv.at[6]).wait()
     gram_row = jnp.broadcast_to(jnp.sum(gram_parts[0], axis=0), (8, LANES))
     entry = {
@@ -595,18 +612,6 @@
     r_out[...] = factor[:, :8] * (1.0 / scale_rows)
     cols_out[...] = remainder * scale_rows
 
-    for copy in halos + coarse_near + [coarse_far] + edges:
-        copy.wait_send()
-    for at in range(3):
-        all_but_one(gathered, at, wide_send.at[at]).wait()
-    all_but_one(norms, 0, wide_send.at[3]).wait()
-    all_but_one(incoming, 0, wide_send.at[4]).wait()
-    pltpu.make_async_copy(
-        proj_parts.at[pl.ds(0, inner - 1)], proj_parts.at[pl.ds(0, inner - 1)], wide_send.at[5]
-    ).wait()
-    pltpu.make_async_copy(
-        proj_sums.at[pl.ds(0, outer - 1)], proj_sums.at[pl.ds(0, outer - 1)], wide_send.at[7]
-    ).wait()
     all_but_one(gram_parts, 0, wide_send.at[6]).wait()
 
 
@@ -655,13 +660,14 @@
                 pltpu.VMEM(vel_now.shape, f32),
                 pltpu.VMEM(acc_now.shape, f32),
                 pltpu.VMEM(load_next.shape, f32),
-                pltpu.VMEM((2, width, coarse_inverse.shape[1]), jnp.bfloat16),
-                pltpu.VMEM((2, width, width + 2 * NI), jnp.bfloat16),
+                pltpu.VMEM((2, coarse_inverse.shape[1], width), jnp.bfloat16),
+                pltpu.VMEM((2, width, (sub_count + 4) * NI), jnp.bfloat16),
                 pltpu.VMEM((2, width, (sub_count + 1) * NI + width), jnp.bfloat16),
                 pltpu.VMEM((2, width, (sub_count + 2) * NI), jnp.bfloat16),
                 pltpu.VMEM((2, width, (sub_count + 1) * NI), jnp.bfloat16),
                 pltpu.VMEM((2, width, sub_count * unknowns), jnp.bfloat16),
                 pltpu.VMEM((2,) + basis_rows.shape, jnp.bfloat16),
+                pltpu.VMEM((2,) + basis_rows.shape[::-1], jnp.bfloat16),
                 pltpu.VMEM(rr_inverse.shape, f32),
                 pltpu.VMEM(corner_modes.shape, f32),
                 pltpu.VMEM((width + NC, coarse_inverse.shape[1]), f32),
@@ -671,8 +677,6 @@
                 pltpu.VMEM((width, sub_count * unknowns), f32),
                 pltpu.VMEM((width, (sub_count + 1) * NI), f32),
                 pltpu.VMEM((width, (sub_count + 1) * NI), f32),
-                pltpu.VMEM((width, (sub_count + 2) * NI), f32),
-                pltpu.VMEM((width, (sub_count + 2) * NI), f32),
                 pltpu.VMEM((3, n, case_count, width), f32),
                 pltpu.VMEM((6, case_count, NI), f32),
                 pltpu.VMEM((6, case_count, NI), f32),

time: 46.6 us -> 45.1 us (0.968)
  Pallas kernels: 45.8 us -> 44.3 us
    pallas_call x1, Pallas kernels: 45.1 us -> 43.7 us  [shards(): pl.pallas_call(functools.partial(kernel, n, groups, inner), out_shape=kep...]
where the time goes in v3:
time: 45.1 us; the launch traced here: 45 us
  Pallas kernels  44.3 us (98%)
  between operations  0.64 us (1%)
    pallas_call x1, Pallas kernels, shards(): pl.pallas_call(functools.partial(kernel, n, groups, inner), out_shape=kep...  43.7 us

profile of v3, /device:TPU:0, one launch (start us, length us, event | category | flops | bytes accessed | tf_op | source)
XLA Modules:
  0.0 45.0 jit_solution(16454877993841761949)
XLA Ops:
  0.6 43.7 %shard_map.137 = (f32[8,2,512]{2,1,0:T(2,128)S(1)}, f32[8,2,512]{2,1,0:T(2,128)S(1)}, f32[8,256]{1,0:T(8,128)S(1)}, f32[8,8]{1,0:T(8,128)S(1)}, f32[8,1024]{1,0:T(8,128)S(1)}) custom-call(s32[32]{0:T(128)} %owner_hbm.1, f32[2,512,512]{2,1,0:T(8,128)} %rr_hbm.1, f32[2,64,512]{2,1,0:T(8,128)} %modes_hbm.1, f32[64,2048]{1,0:T(8,128)} %coarse_hbm.1, ...), custom_call_target="tpu_custom_call" | custom-call | tf_op jit(solution)/shard_map/pallas_call | solution.py:650
  44.3 0.7 %shard_map.138 = (f32[8,2,512]{2,1,0:T(2,128)}, f32[8,2,512]{2,1,0:T(2,128)}, f32[8,256]{1,0:T(8,128)}, f32[8,8]{1,0:T(8,128)}, f32[8,1024]{1,0:T(8,128)}) custom-call(f32[8,2,512]{2,1,0:T(2,128)S(1)} %get-tuple-element.15.refs_0_, f32[8,2,512]{2,1,0:T(2,128)S(1)} %get-tuple-element.16.refs_1_, f32[8,256]{1,0:T(8,128)S(1)} %get-tuple-element.17.refs_2_, ...), custom_call_target="tpu_custom_call" | custom-call | tf_op jit(solution)/shard_map/pallas_call | solution.py:712

commit v4 on v3

--- a/solution.py
+++ b/solution.py
@@ -139,7 +139,14 @@
 
     plane, outer = me // inner, n // inner
     seat = lax.rem(me, inner)
-    seats = [lax.rem(2 * inner - 1 - seat + i, inner) for i in range(inner)]
+    bits = inner.bit_length() - 1
+
+    def flipped(mask):
+        parts = [lax.rem(seat // 2**bit + mask // 2**bit, 2) * 2**bit for bit in range(bits)]
+        return sum(parts[1:], parts[0]) if parts else seat
+
+    masks = sorted(range(inner), key=lambda mask: (-mask.bit_count(), -mask))
+    seats = [flipped(mask) for mask in masks]
     mirrored = 2 * plane > outer - 1
     depth = jnp.where(mirrored, outer - 1 - plane, plane)
     lead = outer - 1 - 2 * depth
@@ -155,8 +162,8 @@
             return carry
 
         lax.fori_loop(0, outer - 1, step, 0)
-        for i in range(1, inner):
-            body(plane * inner + lax.rem(seat + i, inner))
+        for there in seats[:-1]:
+            body(plane * inner + there)
 
     def remote(src, dst, send, recv, rank):
         return pltpu.make_async_remote_copy(
@@ -540,8 +547,8 @@
         snapshot_tiles.append(total)
     snapshots = jnp.concatenate(snapshot_tiles, axis=1)
     proj_parts[seat] = split_dot(snapshots, basis_parts, 0)
-    for i in range(1, inner):
-        rank = plane * inner + lax.rem(seat + i, inner)
+    for there in seats[:-1]:
+        rank = plane * inner + there
         remote(proj_parts.at[seat], proj_parts.at[seat], wide_send.at[5], wide_recv.at[5], rank).start()
 
     for copy in halos + coarse_near + [coarse_far] + edges:

time: 45.1 us -> 44.2 us (0.980)
  Pallas kernels: 44.3 us -> 43.4 us
    pallas_call x1, Pallas kernels: 43.7 us -> 42.7 us  [shards(): pl.pallas_call(functools.partial(kernel, n, groups, inner), out_shape=kep...]
where the time goes in v4:
time: 44.2 us; the launch traced here: 44 us
  Pallas kernels  43.4 us (98%)
  between operations  0.64 us (1%)
    pallas_call x1, Pallas kernels, shards(): pl.pallas_call(functools.partial(kernel, n, groups, inner), out_shape=kep...  42.7 us

profile of v4, /device:TPU:0, one launch (start us, length us, event | category | flops | bytes accessed | tf_op | source)
XLA Modules:
  0.0 44.0 jit_solution(8464530270262955164)
XLA Ops:
  0.6 42.7 %shard_map.137 = (f32[8,2,512]{2,1,0:T(2,128)S(1)}, f32[8,2,512]{2,1,0:T(2,128)S(1)}, f32[8,256]{1,0:T(8,128)S(1)}, f32[8,8]{1,0:T(8,128)S(1)}, f32[8,1024]{1,0:T(8,128)S(1)}) custom-call(s32[32]{0:T(128)} %owner_hbm.1, f32[2,512,512]{2,1,0:T(8,128)} %rr_hbm.1, f32[2,64,512]{2,1,0:T(8,128)} %modes_hbm.1, f32[64,2048]{1,0:T(8,128)} %coarse_hbm.1, ...), custom_call_target="tpu_custom_call" | custom-call | tf_op jit(solution)/shard_map/pallas_call | solution.py:657
  43.4 0.7 %shard_map.138 = (f32[8,2,512]{2,1,0:T(2,128)}, f32[8,2,512]{2,1,0:T(2,128)}, f32[8,256]{1,0:T(8,128)}, f32[8,8]{1,0:T(8,128)}, f32[8,1024]{1,0:T(8,128)}) custom-call(f32[8,2,512]{2,1,0:T(2,128)S(1)} %get-tuple-element.15.refs_0_, f32[8,2,512]{2,1,0:T(2,128)S(1)} %get-tuple-element.16.refs_1_, f32[8,256]{1,0:T(8,128)S(1)} %get-tuple-element.17.refs_2_, ...), custom_call_target="tpu_custom_call" | custom-call | tf_op jit(solution)/shard_map/pallas_call | solution.py:719
